TPU v7x, 8 devices: a whole 2x2x1 slice. The times are simulated.
8 devices in a mesh: data: 8 (over z, y, x, core).
Axes of the slice: x: 2, y: 2, z: 1, core: 2. Of those that a mesh axis runs over, the one named last changes fastest.
Arguments:
- feat_img: bfloat16 [16384, 768], P('data')
- feat_txt: bfloat16 [16384, 512], P('data')
- w_img: bfloat16 [768, 512], replicated
- w_txt: bfloat16 [512, 512], replicated
- log_temp: float32 [], replicated
- logit_bias: float32 [], replicated
- pair_ids: int32 [16384], P('data')
Outputs:
- output 1: float32 [], replicated
- output 2: float32 [], replicated
- output 3: float32 [], replicated
- output 4: float32 [768, 512], replicated
- output 5: float32 [512, 512], replicated
All inputs are finite; a program needn't handle non-finite values.
Results may differ from a plain program's by a relative error of at most 0.001.
Values are sent between devices in bfloat16 or wider.
A program may use at most 1 GiB of HBM per device.

v0:
```python
import jax
import jax.numpy as jnp
from jax import lax
from jax.sharding import PartitionSpec as P

CONTRACT_ROWS = (((0,), (0,)), ((), ()))
CONTRACT_COLS = (((1,), (1,)), ((), ()))


def embed_rows(feat_rows, weights):
    raw_emb = jnp.dot(feat_rows, weights, preferred_element_type=jnp.float32)
    inv_norm = lax.rsqrt(jnp.sum(raw_emb * raw_emb, axis=1, keepdims=True))
    unit_emb = raw_emb * inv_norm
    return unit_emb, inv_norm, unit_emb.astype(jnp.bfloat16)


def weight_grad(feat_rows, unit_emb, inv_norm, grad_emb):
    raw_grad = inv_norm * (grad_emb - unit_emb * jnp.sum(unit_emb * grad_emb, axis=1, keepdims=True))
    return lax.dot_general(feat_rows, raw_grad.astype(jnp.bfloat16), CONTRACT_ROWS, preferred_element_type=jnp.float32)


def tile_terms(emb_img, ids_img, emb_txt, ids_txt, temp_scale, logit_bias, total_rows):
    sim_tile = lax.dot_general(emb_img, emb_txt, CONTRACT_COLS, preferred_element_type=jnp.float32)
    label_sign = jnp.where(ids_img[:, None] == ids_txt[None, :], 1.0, -1.0).astype(jnp.float32)
    margin = -label_sign * (temp_scale * sim_tile + logit_bias)
    grad_tile = -label_sign * jax.nn.sigmoid(margin) / total_rows
    grad_bf = grad_tile.astype(jnp.bfloat16)
    part_img = jnp.dot(grad_bf, emb_txt, preferred_element_type=jnp.float32)
    part_txt = lax.dot_general(grad_bf, emb_img, CONTRACT_ROWS, preferred_element_type=jnp.float32)
    loss_part = jnp.sum(jax.nn.softplus(margin))
    return part_img, part_txt, loss_part, jnp.sum(grad_tile * sim_tile), jnp.sum(grad_tile)


def solution(mesh):
    n_dev = mesh.shape["data"]
    next_perm = [(src_dev, (src_dev + 1) % n_dev) for src_dev in range(n_dev)]

    def local_fn(feat_img, feat_txt, w_img, w_txt, log_temp, logit_bias, pair_ids):
        total_rows = feat_img.shape[0] * n_dev
        temp_scale = jnp.exp(log_temp)
        unit_img, inv_img, emb_img = embed_rows(feat_img, w_img)
        unit_txt, inv_txt, emb_txt = embed_rows(feat_txt, w_txt)

        def visit_block(hop_index, loop_state):
            txt_blk, ids_blk, acc_txt, acc_img, loss_sum, temp_sum, bias_sum = loop_state
            part_img, part_txt, loss_part, temp_part, bias_part = tile_terms(
                emb_img, pair_ids, txt_blk, ids_blk, temp_scale, logit_bias, total_rows)
            txt_blk, ids_blk, acc_txt = lax.ppermute((txt_blk, ids_blk, acc_txt + part_txt), "data", next_perm)
            return (txt_blk, ids_blk, acc_txt, acc_img + part_img,
                    loss_sum + loss_part, temp_sum + temp_part, bias_sum + bias_part)

        zero_rows = jnp.zeros(emb_img.shape, jnp.float32)
        zero_sum = jnp.zeros((), jnp.float32)
        loop_state = (emb_txt, pair_ids, zero_rows, zero_rows, zero_sum, zero_sum, zero_sum)
        loop_state = lax.fori_loop(0, n_dev - 1, visit_block, loop_state)
        txt_blk, ids_blk, acc_txt, acc_img, loss_sum, temp_sum, bias_sum = loop_state
        part_img, part_txt, loss_part, temp_part, bias_part = tile_terms(
            emb_img, pair_ids, txt_blk, ids_blk, temp_scale, logit_bias, total_rows)
        home_txt = lax.ppermute(acc_txt + part_txt, "data", next_perm)
        grad_img = temp_scale * (acc_img + part_img)
        grad_txt = temp_scale * home_txt
        dw_img = weight_grad(feat_img, unit_img, inv_img, grad_img)
        dw_txt = weight_grad(feat_txt, unit_txt, inv_txt, grad_txt)
        totals = lax.psum((loss_sum + loss_part, temp_sum + temp_part, bias_sum + bias_part, dw_img, dw_txt), "data")
        return totals[0] / total_rows, temp_scale * totals[1], totals[2], totals[3], totals[4]

    return jax.shard_map(
        local_fn,
        mesh=mesh,
        in_specs=(P("data", None), P("data", None), P(None, None), P(None, None), P(), P(), P("data")),
        out_specs=(P(), P(), P(), P(None, None), P(None, None)),
        check_vma=False,
    )
```

profile of v0, /device:TPU:0, one launch (start us, length us, event | category | flops | bytes accessed | tf_op | source)
XLA Modules:
  0.0 954.7 jit_solution(2585704067720460750)
XLA Ops:
  7.2 1.8 copy-done
  9.1 3.0 multiply_reduce_fusion.4
  12.1 1.9 copy-done.5
  14.0 1.9 multiply_convert_fusion.2
  15.9 3.9 copy.13
  19.8 3.0 multiply_reduce_fusion.5
  22.8 1.9 copy-done.1
  24.8 1.8 multiply_convert_fusion.3
  26.6 3.9 copy.12
  31.9 2.5 broadcast_in_dim.25
  34.4 758.7 %while.23 = (s32[]{:T(128)}, bf16[2048,512]{1,0:T(8,128)(2,1)}, s32[2048]{0:T(1024)S(1)}, f32[2048,512]{1,0:T(8,128)}, f32[2048,512]{1,0:T(8,128)}, /*index=5*/f...) while((s32[]{:T(128)}, bf16[2048,512]{1,0:T(8,128)(2,1)}, ...), condition=%wide.region_6.7_spmd.clone, body=%wide.region_2.6_spmd.clone.sunk | while | flops 12980322304 | bytes 121700728 | solution.py:55
  34.4 3.2 copy.29
  37.6 24.4 %fusion.63 = (f32[]{:T(128)}, f32[]{:T(128)}, f32[]{:T(128)}, bf16[2048,2048]{1,0:T(8,128)(2,1)S(1)}) fusion(f32[]{:T(128)} %get-tuple-element.307, f32[]{:T(128)} %get-tuple-element.305, s32[2048]{0:T(1024)S(1)} %copy.30, s32[2048]{0:T(1024)S(1)} %get-tuple-element.304, bf16[2048,512]{1,0:T(8,128)(2,1)S(1)} %copy-done.8, bf16[2048,512]{1,0:T(8,128)(2,1)} %copy.29), kind=kOutput, calls=%fused_computation.41.clone.1 | convolution fusion | flops 4387241984 | bytes 12599316 | tf_op jit(solution)/shard_map/while/body/eval_jaxpr/dot_general | solution.py:23
  62.0 9.2 fusion.64
  71.2 0.9 collective-permute-start.2
  72.1 2.6 collective-permute-start
  74.7 10.4 %select_add_fusion.2 = f32[2048,512]{1,0:T(8,128)} fusion(f32[2048,512]{1,0:T(8,128)} %get-tuple-element.286, bf16[2048,512]{1,0:T(8,128)(2,1)} %copy.29, bf16[2048,2048]{1,0:T(8,128)(2,1)} %copy-done.15, pred[]{:T(512)S(6)} %compare.3), kind=kOutput, calls=%fused_computation.6.clone.1 | convolution fusion | flops 4297064448 | bytes 18874368 | tf_op jit(solution)/shard_map/while/body/eval_jaxpr/dot_general | solution.py:28
  87.0 56.7 %collective-permute-done.1 = s32[2048]{0:T(1024)S(1)} collective-permute-done((s32[2048]{0:T(1024)S(1)}, s32[2048]{0:T(1024)S(1)}, u32[]{:S(2)}, u32[]{:S(2)}) %collective-permute-start.1) | collective-permute-done | bytes 8224 | tf_op jit(solution)/shard_map/while/body/eval_jaxpr/ppermute | solution.py:48
  143.7 3.2 copy.29
  146.9 24.4 %fusion.63 = (f32[]{:T(128)}, f32[]{:T(128)}, f32[]{:T(128)}, bf16[2048,2048]{1,0:T(8,128)(2,1)S(1)}) fusion(f32[]{:T(128)} %get-tuple-element.307, f32[]{:T(128)} %get-tuple-element.305, s32[2048]{0:T(1024)S(1)} %copy.30, s32[2048]{0:T(1024)S(1)} %get-tuple-element.304, bf16[2048,512]{1,0:T(8,128)(2,1)S(1)} %copy-done.8, bf16[2048,512]{1,0:T(8,128)(2,1)} %copy.29), kind=kOutput, calls=%fused_computation.41.clone.1 | convolution fusion | flops 4387241984 | bytes 12599316 | tf_op jit(solution)/shard_map/while/body/eval_jaxpr/dot_general | solution.py:23
  171.3 9.2 fusion.64
  180.5 1.5 collective-permute-start
  182.0 11.6 %select_add_fusion.2 = f32[2048,512]{1,0:T(8,128)} fusion(f32[2048,512]{1,0:T(8,128)} %get-tuple-element.286, bf16[2048,512]{1,0:T(8,128)(2,1)} %copy.29, bf16[2048,2048]{1,0:T(8,128)(2,1)} %copy-done.15, pred[]{:T(512)S(6)} %compare.3), kind=kOutput, calls=%fused_computation.6.clone.1 | convolution fusion | flops 4297064448 | bytes 18874368 | tf_op jit(solution)/shard_map/while/body/eval_jaxpr/dot_general | solution.py:28
  195.5 56.4 %collective-permute-done.1 = s32[2048]{0:T(1024)S(1)} collective-permute-done((s32[2048]{0:T(1024)S(1)}, s32[2048]{0:T(1024)S(1)}, u32[]{:S(2)}, u32[]{:S(2)}) %collective-permute-start.1) | collective-permute-done | bytes 8224 | tf_op jit(solution)/shard_map/while/body/eval_jaxpr/ppermute | solution.py:48
  251.9 3.2 copy.29
  255.1 24.4 %fusion.63 = (f32[]{:T(128)}, f32[]{:T(128)}, f32[]{:T(128)}, bf16[2048,2048]{1,0:T(8,128)(2,1)S(1)}) fusion(f32[]{:T(128)} %get-tuple-element.307, f32[]{:T(128)} %get-tuple-element.305, s32[2048]{0:T(1024)S(1)} %copy.30, s32[2048]{0:T(1024)S(1)} %get-tuple-element.304, bf16[2048,512]{1,0:T(8,128)(2,1)S(1)} %copy-done.8, bf16[2048,512]{1,0:T(8,128)(2,1)} %copy.29), kind=kOutput, calls=%fused_computation.41.clone.1 | convolution fusion | flops 4387241984 | bytes 12599316 | tf_op jit(solution)/shard_map/while/body/eval_jaxpr/dot_general | solution.py:23
  279.5 9.2 fusion.64
  288.8 0.6 collective-permute-start
  289.3 11.6 %select_add_fusion.2 = f32[2048,512]{1,0:T(8,128)} fusion(f32[2048,512]{1,0:T(8,128)} %get-tuple-element.286, bf16[2048,512]{1,0:T(8,128)(2,1)} %copy.29, bf16[2048,2048]{1,0:T(8,128)(2,1)} %copy-done.15, pred[]{:T(512)S(6)} %compare.3), kind=kOutput, calls=%fused_computation.6.clone.1 | convolution fusion | flops 4297064448 | bytes 18874368 | tf_op jit(solution)/shard_map/while/body/eval_jaxpr/dot_general | solution.py:28
  302.8 57.3 %collective-permute-done.1 = s32[2048]{0:T(1024)S(1)} collective-permute-done((s32[2048]{0:T(1024)S(1)}, s32[2048]{0:T(1024)S(1)}, u32[]{:S(2)}, u32[]{:S(2)}) %collective-permute-start.1) | collective-permute-done | bytes 8224 | tf_op jit(solution)/shard_map/while/body/eval_jaxpr/ppermute | solution.py:48
  360.2 3.2 copy.29
  363.4 24.4 %fusion.63 = (f32[]{:T(128)}, f32[]{:T(128)}, f32[]{:T(128)}, bf16[2048,2048]{1,0:T(8,128)(2,1)S(1)}) fusion(f32[]{:T(128)} %get-tuple-element.307, f32[]{:T(128)} %get-tuple-element.305, s32[2048]{0:T(1024)S(1)} %copy.30, s32[2048]{0:T(1024)S(1)} %get-tuple-element.304, bf16[2048,512]{1,0:T(8,128)(2,1)S(1)} %copy-done.8, bf16[2048,512]{1,0:T(8,128)(2,1)} %copy.29), kind=kOutput, calls=%fused_computation.41.clone.1 | convolution fusion | flops 4387241984 | bytes 12599316 | tf_op jit(solution)/shard_map/while/body/eval_jaxpr/dot_general | solution.py:23
  387.8 9.2 fusion.64
  397.0 0.6 collective-permute-start.1
  397.6 11.6 %select_add_fusion.2 = f32[2048,512]{1,0:T(8,128)} fusion(f32[2048,512]{1,0:T(8,128)} %get-tuple-element.286, bf16[2048,512]{1,0:T(8,128)(2,1)} %copy.29, bf16[2048,2048]{1,0:T(8,128)(2,1)} %copy-done.15, pred[]{:T(512)S(6)} %compare.3), kind=kOutput, calls=%fused_computation.6.clone.1 | convolution fusion | flops 4297064448 | bytes 18874368 | tf_op jit(solution)/shard_map/while/body/eval_jaxpr/dot_general | solution.py:28
  411.0 57.4 %collective-permute-done.1 = s32[2048]{0:T(1024)S(1)} collective-permute-done((s32[2048]{0:T(1024)S(1)}, s32[2048]{0:T(1024)S(1)}, u32[]{:S(2)}, u32[]{:S(2)}) %collective-permute-start.1) | collective-permute-done | bytes 8224 | tf_op jit(solution)/shard_map/while/body/eval_jaxpr/ppermute | solution.py:48
  468.4 3.2 copy.29
  471.6 24.4 %fusion.63 = (f32[]{:T(128)}, f32[]{:T(128)}, f32[]{:T(128)}, bf16[2048,2048]{1,0:T(8,128)(2,1)S(1)}) fusion(f32[]{:T(128)} %get-tuple-element.307, f32[]{:T(128)} %get-tuple-element.305, s32[2048]{0:T(1024)S(1)} %copy.30, s32[2048]{0:T(1024)S(1)} %get-tuple-element.304, bf16[2048,512]{1,0:T(8,128)(2,1)S(1)} %copy-done.8, bf16[2048,512]{1,0:T(8,128)(2,1)} %copy.29), kind=kOutput, calls=%fused_computation.41.clone.1 | convolution fusion | flops 4387241984 | bytes 12599316 | tf_op jit(solution)/shard_map/while/body/eval_jaxpr/dot_general | solution.py:23
  496.0 9.2 fusion.64
  505.8 11.6 %select_add_fusion.2 = f32[2048,512]{1,0:T(8,128)} fusion(f32[2048,512]{1,0:T(8,128)} %get-tuple-element.286, bf16[2048,512]{1,0:T(8,128)(2,1)} %copy.29, bf16[2048,2048]{1,0:T(8,128)(2,1)} %copy-done.15, pred[]{:T(512)S(6)} %compare.3), kind=kOutput, calls=%fused_computation.6.clone.1 | convolution fusion | flops 4297064448 | bytes 18874368 | tf_op jit(solution)/shard_map/while/body/eval_jaxpr/dot_general | solution.py:28
  519.2 57.4 %collective-permute-done.1 = s32[2048]{0:T(1024)S(1)} collective-permute-done((s32[2048]{0:T(1024)S(1)}, s32[2048]{0:T(1024)S(1)}, u32[]{:S(2)}, u32[]{:S(2)}) %collective-permute-start.1) | collective-permute-done | bytes 8224 | tf_op jit(solution)/shard_map/while/body/eval_jaxpr/ppermute | solution.py:48
  576.6 3.2 copy.29
  579.8 24.4 %fusion.63 = (f32[]{:T(128)}, f32[]{:T(128)}, f32[]{:T(128)}, bf16[2048,2048]{1,0:T(8,128)(2,1)S(1)}) fusion(f32[]{:T(128)} %get-tuple-element.307, f32[]{:T(128)} %get-tuple-element.305, s32[2048]{0:T(1024)S(1)} %copy.30, s32[2048]{0:T(1024)S(1)} %get-tuple-element.304, bf16[2048,512]{1,0:T(8,128)(2,1)S(1)} %copy-done.8, bf16[2048,512]{1,0:T(8,128)(2,1)} %copy.29), kind=kOutput, calls=%fused_computation.41.clone.1 | convolution fusion | flops 4387241984 | bytes 12599316 | tf_op jit(solution)/shard_map/while/body/eval_jaxpr/dot_general | solution.py:23
  604.2 9.2 fusion.64
  614.0 11.6 %select_add_fusion.2 = f32[2048,512]{1,0:T(8,128)} fusion(f32[2048,512]{1,0:T(8,128)} %get-tuple-element.286, bf16[2048,512]{1,0:T(8,128)(2,1)} %copy.29, bf16[2048,2048]{1,0:T(8,128)(2,1)} %copy-done.15, pred[]{:T(512)S(6)} %compare.3), kind=kOutput, calls=%fused_computation.6.clone.1 | convolution fusion | flops 4297064448 | bytes 18874368 | tf_op jit(solution)/shard_map/while/body/eval_jaxpr/dot_general | solution.py:28
  627.5 57.4 %collective-permute-done.1 = s32[2048]{0:T(1024)S(1)} collective-permute-done((s32[2048]{0:T(1024)S(1)}, s32[2048]{0:T(1024)S(1)}, u32[]{:S(2)}, u32[]{:S(2)}) %collective-permute-start.1) | collective-permute-done | bytes 8224 | tf_op jit(solution)/shard_map/while/body/eval_jaxpr/ppermute | solution.py:48
  684.8 3.2 copy.29
  688.0 24.4 %fusion.63 = (f32[]{:T(128)}, f32[]{:T(128)}, f32[]{:T(128)}, bf16[2048,2048]{1,0:T(8,128)(2,1)S(1)}) fusion(f32[]{:T(128)} %get-tuple-element.307, f32[]{:T(128)} %get-tuple-element.305, s32[2048]{0:T(1024)S(1)} %copy.30, s32[2048]{0:T(1024)S(1)} %get-tuple-element.304, bf16[2048,512]{1,0:T(8,128)(2,1)S(1)} %copy-done.8, bf16[2048,512]{1,0:T(8,128)(2,1)} %copy.29), kind=kOutput, calls=%fused_computation.41.clone.1 | convolution fusion | flops 4387241984 | bytes 12599316 | tf_op jit(solution)/shard_map/while/body/eval_jaxpr/dot_general | solution.py:23
  712.5 9.2 fusion.64
  722.2 11.6 %select_add_fusion.2 = f32[2048,512]{1,0:T(8,128)} fusion(f32[2048,512]{1,0:T(8,128)} %get-tuple-element.286, bf16[2048,512]{1,0:T(8,128)(2,1)} %copy.29, bf16[2048,2048]{1,0:T(8,128)(2,1)} %copy-done.15, pred[]{:T(512)S(6)} %compare.3), kind=kOutput, calls=%fused_computation.6.clone.1 | convolution fusion | flops 4297064448 | bytes 18874368 | tf_op jit(solution)/shard_map/while/body/eval_jaxpr/dot_general | solution.py:28
  735.7 57.4 %collective-permute-done.1 = s32[2048]{0:T(1024)S(1)} collective-permute-done((s32[2048]{0:T(1024)S(1)}, s32[2048]{0:T(1024)S(1)}, u32[]{:S(2)}, u32[]{:S(2)}) %collective-permute-start.1) | collective-permute-done | bytes 8224 | tf_op jit(solution)/shard_map/while/body/eval_jaxpr/ppermute | solution.py:48
  793.1 5.4 copy.15
  798.5 23.5 %fusion.30 = (f32[]{:T(128)}, f32[]{:T(128)}, f32[]{:T(128)}, bf16[2048,2048]{1,0:T(8,128)(2,1)S(1)}) fusion(f32[]{:T(128)S(6)} %copy.48, f32[]{:T(128)} %exp.16, s32[2048]{0:T(1024)S(1)} %get-tuple-element.74, s32[2048]{0:T(1024)S(1)} %get-tuple-element.322, bf16[2048,512]{0,1:T(8,128)(2,1)} %multiply_convert_fusion.2, bf16[2048,512]{1,0:T(8,128)(2,1)} %get-tuple-element.75), kind=kOutput, calls=%fused_computation.42 | convolution fusion | flops 4387241984 | bytes 12599316 | tf_op jit(solution)/shard_map/dot_general | solution.py:23
  822.0 6.1 fusion.17
  828.1 5.4 copy.14
  833.5 11.6 %multiply_reduce_fusion.3 = (f32[2048]{0:T(1024)S(1)}, f32[2048,512]{0,1:T(8,128)S(1)}) fusion(f32[2048,512]{0,1:T(8,128)} %copy-done.5, f32[2048]{0:T(1024)S(1)} %copy-done.12, f32[2048,512]{0,1:T(8,128)} %copy.14, bf16[2048,512]{1,0:T(8,128)(2,1)} %get-tuple-element.75, bf16[2048,2048]{1,0:T(8,128)(2,1)} %copy-done.14, f32[]{:T(128)} %exp.16), kind=kOutput, calls=%fused_computation.21 | convolution fusion | flops 4300208128 | bytes 23085060 | tf_op jit(solution)/shard_map/dot_general | solution.py:28
  845.1 3.1 fusion.27
  848.2 28.7 %collective-permute-done.3 = f32[2048,512]{0,1:T(8,128)} collective-permute-done((f32[2048,512]{0,1:T(8,128)}, f32[2048,512]{0,1:T(8,128)}, u32[]{:S(2)}, u32[]{:S(2)}) %collective-permute-start.3) | collective-permute-done | bytes 4194336 | tf_op jit(solution)/shard_map/ppermute | solution.py:59
  877.0 3.0 multiply_reduce_fusion.2
  880.0 4.5 fusion.28
  886.5 22.8 %all-reduce = (f32[]{:T(128)}, f32[]{:T(128)}, f32[]{:T(128)}) all-reduce(f32[]{:T(128)S(6)} %add.71, f32[]{:T(128)S(6)} %add.73, f32[]{:T(128)S(6)} %add.74), channel_id=1, replica_groups=mesh['data'=8] {'data'}, use_global_device_ids=true, to_apply=%region_8.9 | all-reduce | flops 3 | bytes 24 | tf_op jit(solution)/shard_map/psum | solution.py:64
  910.6 29.5 %all-reduce.4.cloned.1.call-done = (f32[768,512]{0,1:T(8,128)}, f32[512,512]{0,1:T(8,128)}) async-done(((f32[768,512]{0,1:T(8,128)}, f32[512,512]{0,1:T(8,128)}), (f32[768,512]{0,1:T(8,128)}, f32[512,512]{0,1:T(8,128)})) %all-reduce.4.cloned.1.call-update) | async-done | bytes 2621456 | tf_op jit(solution)/shard_map/psum | solution.py:64
  940.1 3.0 copy.17
  943.1 2.5 copy.18
  (97 shorter events, 2.0 us)
Async XLA Ops:
  7.2 1.9 copy-start
  7.2 932.9 %all-reduce.4.cloned.1.call-start = ((), (), s32[]{:S(2)}) async-start(), calls=%async_computation | async-start | bytes 5242880 | tf_op jit(solution)/shard_map/psum | solution.py:64
  12.1 2.0 copy-start.5
  12.1 2.0 copy-start.11
  22.8 2.0 copy-start.1
  22.8 1.9 copy-start.9
  24.8 6.4 copy-start.13
  34.4 3.2 copy-start.8
  62.0 9.2 copy-start.15
  71.2 72.5 %collective-permute-start.2 = (f32[2048,512]{1,0:T(8,128)}, f32[2048,512]{1,0:T(8,128)}, u32[]{:S(2)}, u32[]{:S(2)}) collective-permute-start(f32[2048,512]{1,0:T(8,128)} %fusion.64), channel_id=1, source_target_pairs={{0,1},{1,2},{2,3},{3,4},{4,5},{5,6},{6,7},{7,0}} | collective-permute-start | bytes 12582920 | tf_op jit(solution)/shard_map/while/body/eval_jaxpr/ppermute | solution.py:48
  72.1 71.6 %collective-permute-start = (bf16[2048,512]{1,0:T(8,128)(2,1)}, bf16[2048,512]{1,0:T(8,128)(2,1)}, u32[]{:S(2)}, u32[]{:S(2)}) collective-permute-start(bf16[2048,512]{1,0:T(8,128)(2,1)} %copy.29), channel_id=1, source_target_pairs={{0,1},{1,2},{2,3},{3,4},{4,5},{5,6},{6,7},{7,0}} | collective-permute-start | bytes 6291464 | tf_op jit(solution)/shard_map/while/body/eval_jaxpr/ppermute | solution.py:48
  74.7 69.0 %collective-permute-start.1 = (s32[2048]{0:T(1024)S(1)}, s32[2048]{0:T(1024)S(1)}, u32[]{:S(2)}, u32[]{:S(2)}) collective-permute-start(s32[2048]{0:T(1024)S(1)} %copy.30), channel_id=1, source_target_pairs={{0,1},{1,2},{2,3},{3,4},{4,5},{5,6},{6,7},{7,0}} | collective-permute-start | bytes 24584 | tf_op jit(solution)/shard_map/while/body/eval_jaxpr/ppermute | solution.py:48
  143.7 3.2 copy-start.8
  171.3 9.2 copy-start.15
  180.5 71.4 %collective-permute-start.2 = (f32[2048,512]{1,0:T(8,128)}, f32[2048,512]{1,0:T(8,128)}, u32[]{:S(2)}, u32[]{:S(2)}) collective-permute-start(f32[2048,512]{1,0:T(8,128)} %fusion.64), channel_id=1, source_target_pairs={{0,1},{1,2},{2,3},{3,4},{4,5},{5,6},{6,7},{7,0}} | collective-permute-start | bytes 12582920 | tf_op jit(solution)/shard_map/while/body/eval_jaxpr/ppermute | solution.py:48
  180.5 71.4 %collective-permute-start = (bf16[2048,512]{1,0:T(8,128)(2,1)}, bf16[2048,512]{1,0:T(8,128)(2,1)}, u32[]{:S(2)}, u32[]{:S(2)}) collective-permute-start(bf16[2048,512]{1,0:T(8,128)(2,1)} %copy.29), channel_id=1, source_target_pairs={{0,1},{1,2},{2,3},{3,4},{4,5},{5,6},{6,7},{7,0}} | collective-permute-start | bytes 6291464 | tf_op jit(solution)/shard_map/while/body/eval_jaxpr/ppermute | solution.py:48
  182.0 69.9 %collective-permute-start.1 = (s32[2048]{0:T(1024)S(1)}, s32[2048]{0:T(1024)S(1)}, u32[]{:S(2)}, u32[]{:S(2)}) collective-permute-start(s32[2048]{0:T(1024)S(1)} %copy.30), channel_id=1, source_target_pairs={{0,1},{1,2},{2,3},{3,4},{4,5},{5,6},{6,7},{7,0}} | collective-permute-start | bytes 24584 | tf_op jit(solution)/shard_map/while/body/eval_jaxpr/ppermute | solution.py:48
  251.9 3.2 copy-start.8
  279.5 9.2 copy-start.15
  288.8 71.4 %collective-permute-start.2 = (f32[2048,512]{1,0:T(8,128)}, f32[2048,512]{1,0:T(8,128)}, u32[]{:S(2)}, u32[]{:S(2)}) collective-permute-start(f32[2048,512]{1,0:T(8,128)} %fusion.64), channel_id=1, source_target_pairs={{0,1},{1,2},{2,3},{3,4},{4,5},{5,6},{6,7},{7,0}} | collective-permute-start | bytes 12582920 | tf_op jit(solution)/shard_map/while/body/eval_jaxpr/ppermute | solution.py:48
  288.8 71.4 %collective-permute-start = (bf16[2048,512]{1,0:T(8,128)(2,1)}, bf16[2048,512]{1,0:T(8,128)(2,1)}, u32[]{:S(2)}, u32[]{:S(2)}) collective-permute-start(bf16[2048,512]{1,0:T(8,128)(2,1)} %copy.29), channel_id=1, source_target_pairs={{0,1},{1,2},{2,3},{3,4},{4,5},{5,6},{6,7},{7,0}} | collective-permute-start | bytes 6291464 | tf_op jit(solution)/shard_map/while/body/eval_jaxpr/ppermute | solution.py:48
  289.3 70.8 %collective-permute-start.1 = (s32[2048]{0:T(1024)S(1)}, s32[2048]{0:T(1024)S(1)}, u32[]{:S(2)}, u32[]{:S(2)}) collective-permute-start(s32[2048]{0:T(1024)S(1)} %copy.30), channel_id=1, source_target_pairs={{0,1},{1,2},{2,3},{3,4},{4,5},{5,6},{6,7},{7,0}} | collective-permute-start | bytes 24584 | tf_op jit(solution)/shard_map/while/body/eval_jaxpr/ppermute | solution.py:48
  360.2 3.2 copy-start.8
  387.8 9.2 copy-start.15
  397.0 71.4 %collective-permute-start.2 = (f32[2048,512]{1,0:T(8,128)}, f32[2048,512]{1,0:T(8,128)}, u32[]{:S(2)}, u32[]{:S(2)}) collective-permute-start(f32[2048,512]{1,0:T(8,128)} %fusion.64), channel_id=1, source_target_pairs={{0,1},{1,2},{2,3},{3,4},{4,5},{5,6},{6,7},{7,0}} | collective-permute-start | bytes 12582920 | tf_op jit(solution)/shard_map/while/body/eval_jaxpr/ppermute | solution.py:48
  397.0 71.4 %collective-permute-start = (bf16[2048,512]{1,0:T(8,128)(2,1)}, bf16[2048,512]{1,0:T(8,128)(2,1)}, u32[]{:S(2)}, u32[]{:S(2)}) collective-permute-start(bf16[2048,512]{1,0:T(8,128)(2,1)} %copy.29), channel_id=1, source_target_pairs={{0,1},{1,2},{2,3},{3,4},{4,5},{5,6},{6,7},{7,0}} | collective-permute-start | bytes 6291464 | tf_op jit(solution)/shard_map/while/body/eval_jaxpr/ppermute | solution.py:48
  397.0 71.4 %collective-permute-start.1 = (s32[2048]{0:T(1024)S(1)}, s32[2048]{0:T(1024)S(1)}, u32[]{:S(2)}, u32[]{:S(2)}) collective-permute-start(s32[2048]{0:T(1024)S(1)} %copy.30), channel_id=1, source_target_pairs={{0,1},{1,2},{2,3},{3,4},{4,5},{5,6},{6,7},{7,0}} | collective-permute-start | bytes 24584 | tf_op jit(solution)/shard_map/while/body/eval_jaxpr/ppermute | solution.py:48
  468.4 3.2 copy-start.8
  496.0 9.2 copy-start.15
  505.2 71.4 %collective-permute-start.2 = (f32[2048,512]{1,0:T(8,128)}, f32[2048,512]{1,0:T(8,128)}, u32[]{:S(2)}, u32[]{:S(2)}) collective-permute-start(f32[2048,512]{1,0:T(8,128)} %fusion.64), channel_id=1, source_target_pairs={{0,1},{1,2},{2,3},{3,4},{4,5},{5,6},{6,7},{7,0}} | collective-permute-start | bytes 12582920 | tf_op jit(solution)/shard_map/while/body/eval_jaxpr/ppermute | solution.py:48
  505.2 71.4 %collective-permute-start = (bf16[2048,512]{1,0:T(8,128)(2,1)}, bf16[2048,512]{1,0:T(8,128)(2,1)}, u32[]{:S(2)}, u32[]{:S(2)}) collective-permute-start(bf16[2048,512]{1,0:T(8,128)(2,1)} %copy.29), channel_id=1, source_target_pairs={{0,1},{1,2},{2,3},{3,4},{4,5},{5,6},{6,7},{7,0}} | collective-permute-start | bytes 6291464 | tf_op jit(solution)/shard_map/while/body/eval_jaxpr/ppermute | solution.py:48
  505.2 71.4 %collective-permute-start.1 = (s32[2048]{0:T(1024)S(1)}, s32[2048]{0:T(1024)S(1)}, u32[]{:S(2)}, u32[]{:S(2)}) collective-permute-start(s32[2048]{0:T(1024)S(1)} %copy.30), channel_id=1, source_target_pairs={{0,1},{1,2},{2,3},{3,4},{4,5},{5,6},{6,7},{7,0}} | collective-permute-start | bytes 24584 | tf_op jit(solution)/shard_map/while/body/eval_jaxpr/ppermute | solution.py:48
  576.6 3.2 copy-start.8
  604.2 9.2 copy-start.15
  613.4 71.4 %collective-permute-start.2 = (f32[2048,512]{1,0:T(8,128)}, f32[2048,512]{1,0:T(8,128)}, u32[]{:S(2)}, u32[]{:S(2)}) collective-permute-start(f32[2048,512]{1,0:T(8,128)} %fusion.64), channel_id=1, source_target_pairs={{0,1},{1,2},{2,3},{3,4},{4,5},{5,6},{6,7},{7,0}} | collective-permute-start | bytes 12582920 | tf_op jit(solution)/shard_map/while/body/eval_jaxpr/ppermute | solution.py:48
  613.4 71.4 %collective-permute-start = (bf16[2048,512]{1,0:T(8,128)(2,1)}, bf16[2048,512]{1,0:T(8,128)(2,1)}, u32[]{:S(2)}, u32[]{:S(2)}) collective-permute-start(bf16[2048,512]{1,0:T(8,128)(2,1)} %copy.29), channel_id=1, source_target_pairs={{0,1},{1,2},{2,3},{3,4},{4,5},{5,6},{6,7},{7,0}} | collective-permute-start | bytes 6291464 | tf_op jit(solution)/shard_map/while/body/eval_jaxpr/ppermute | solution.py:48
  613.5 71.4 %collective-permute-start.1 = (s32[2048]{0:T(1024)S(1)}, s32[2048]{0:T(1024)S(1)}, u32[]{:S(2)}, u32[]{:S(2)}) collective-permute-start(s32[2048]{0:T(1024)S(1)} %copy.30), channel_id=1, source_target_pairs={{0,1},{1,2},{2,3},{3,4},{4,5},{5,6},{6,7},{7,0}} | collective-permute-start | bytes 24584 | tf_op jit(solution)/shard_map/while/body/eval_jaxpr/ppermute | solution.py:48
  684.8 3.2 copy-start.8
  712.5 9.2 copy-start.15
  721.7 71.4 %collective-permute-start.2 = (f32[2048,512]{1,0:T(8,128)}, f32[2048,512]{1,0:T(8,128)}, u32[]{:S(2)}, u32[]{:S(2)}) collective-permute-start(f32[2048,512]{1,0:T(8,128)} %fusion.64), channel_id=1, source_target_pairs={{0,1},{1,2},{2,3},{3,4},{4,5},{5,6},{6,7},{7,0}} | collective-permute-start | bytes 12582920 | tf_op jit(solution)/shard_map/while/body/eval_jaxpr/ppermute | solution.py:48
  721.7 71.4 %collective-permute-start = (bf16[2048,512]{1,0:T(8,128)(2,1)}, bf16[2048,512]{1,0:T(8,128)(2,1)}, u32[]{:S(2)}, u32[]{:S(2)}) collective-permute-start(bf16[2048,512]{1,0:T(8,128)(2,1)} %copy.29), channel_id=1, source_target_pairs={{0,1},{1,2},{2,3},{3,4},{4,5},{5,6},{6,7},{7,0}} | collective-permute-start | bytes 6291464 | tf_op jit(solution)/shard_map/while/body/eval_jaxpr/ppermute | solution.py:48
  721.7 71.4 %collective-permute-start.1 = (s32[2048]{0:T(1024)S(1)}, s32[2048]{0:T(1024)S(1)}, u32[]{:S(2)}, u32[]{:S(2)}) collective-permute-start(s32[2048]{0:T(1024)S(1)} %copy.30), channel_id=1, source_target_pairs={{0,1},{1,2},{2,3},{3,4},{4,5},{5,6},{6,7},{7,0}} | collective-permute-start | bytes 24584 | tf_op jit(solution)/shard_map/while/body/eval_jaxpr/ppermute | solution.py:48
  798.5 23.6 %copy-start.4 = (bf16[2048,512]{0,1:T(8,128)(2,1)S(1)}, bf16[2048,512]{0,1:T(8,128)(2,1)}, u32[]{:S(2)}) copy-start(bf16[2048,512]{0,1:T(8,128)(2,1)} %multiply_convert_fusion.2) | copy-start | bytes 6291460
  798.5 23.6 %copy-start.7 = (f32[2048,512]{0,1:T(8,128)S(1)}, f32[2048,512]{0,1:T(8,128)}, u32[]{:S(2)}) copy-start(f32[2048,512]{0,1:T(8,128)} %copy.15) | copy-start | bytes 12582916
  822.0 6.1 copy-start.14
  828.1 48.8 %collective-permute-start.3 = (f32[2048,512]{0,1:T(8,128)}, f32[2048,512]{0,1:T(8,128)}, u32[]{:S(2)}, u32[]{:S(2)}) collective-permute-start(f32[2048,512]{0,1:T(8,128)} %fusion.17), channel_id=1, source_target_pairs={{0,1},{1,2},{2,3},{3,4},{4,5},{5,6},{6,7},{7,0}} | collective-permute-start | bytes 12582920 | tf_op jit(solution)/shard_map/ppermute | solution.py:59
  828.1 5.4 copy-start.12
  833.5 11.6 %copy-start.6 = (f32[2048,512]{0,1:T(8,128)S(1)}, f32[2048,512]{0,1:T(8,128)}, u32[]{:S(2)}) copy-start(f32[2048,512]{0,1:T(8,128)} %copy-done.5) | copy-start | bytes 12582916
  845.1 31.8 %copy-start.2 = (f32[2048,512]{0,1:T(8,128)S(1)}, f32[2048,512]{0,1:T(8,128)}, u32[]{:S(2)}) copy-start(f32[2048,512]{0,1:T(8,128)} %copy-done.1) | copy-start | bytes 12582916
  845.1 31.8 %copy-start.10 = (f32[2048]{0:T(1024)S(1)}, f32[2048]{0:T(1024)}, u32[]{:S(2)}) copy-start(f32[2048]{0:T(1024)} %copy-done.9) | copy-start | bytes 24580
  848.2 31.8 %copy-start.3 = (bf16[2048,512]{1,0:T(8,128)(2,1)S(1)}, bf16[2048,512]{1,0:T(8,128)(2,1)}, u32[]{:S(2)}) copy-start(bf16[2048,512]{1,0:T(8,128)(2,1)} %param.10) | copy-start | bytes 6291460
Sparse Core Ops, SparseCore 0:
  884.7 55.3 all-reduce.3
where the time goes:
time: 956 us; the launch traced here: 955 us
  waiting for transfers between devices  458 us (48%)
  matrix products  370 us (39%)
  local copies, waits for them, and re-layouts  54.9 us (6%)
  blocking collectives  22.8 us (2%)
  between operations  21 us (2%)
  loops' own time  13 us (1%)
    ppermute x21, waiting for transfers between devices, visit_block(): lax.ppermute((txt_blk, ids_blk, acc_txt + part_txt), 'data', next_perm)  400 us
    dot_general x8, matrix products, tile_terms(): lax.dot_general(emb_img, emb_txt, CONTRACT_COLS, preferred_element_type=j...  194 us
    dot_general x8, matrix products, tile_terms(): part_img = jnp.dot(grad_bf, emb_txt, preferred_element_type=jnp.float32)  91.7 us
    dot_general x8, matrix products, tile_terms(): lax.dot_general(grad_bf, emb_img, CONTRACT_ROWS, preferred_element_type=j...  70.6 us
    psum x1, waiting for transfers between devices, local_fn(): lax.psum((loss_sum + loss_part, temp_sum + temp_part, bias_sum + bias_par...  29.5 us
    ppermute x1, waiting for transfers between devices, local_fn(): home_txt = lax.ppermute(acc_txt + part_txt, 'data', next_perm)  28.7 us
    psum x1, blocking collectives, local_fn(): lax.psum((loss_sum + loss_part, temp_sum + temp_part, bias_sum + bias_par...  22.8 us
    while x42, local copies, waits for them, and re-layouts  22.4 us
  transfers between devices with their start and end apart: 23, of which 9 were waited for; matrix products, arithmetic and copies ran while one was open for 10% of the time, Pallas kernels for 0%

commit v1 on v0

v1 whole, which is shorter than its diff:
```python
import functools

import jax
import jax.numpy as jnp
from jax import lax
from jax.experimental import pallas as pl
from jax.experimental.pallas import tpu as pltpu
from jax.sharding import PartitionSpec as P

CONTRACT_ROWS = (((0,), (0,)), ((), ()))
CONTRACT_COLS = (((1,), (1,)), ((), ()))
F32 = jnp.float32
BF16 = jnp.bfloat16
MESH = pl.DeviceIdType.MESH
LOG2E = 1.4426950408889634
N_DEV = 8
ROW_BLK = 512
COL_BLK = 1024
STRIP = 64

REL_P, REL_X, REL_Y, REL_XP, REL_YP, REL_D, REL_DP = range(7)


def flip_bits(core, cx, cy, fc, fx, fy):
    return (core + fc - 2 * core * fc) + 2 * (cx + fx - 2 * cx * fx) + 4 * (cy + fy - 2 * cy * fy)


def enter(me, peers):
    barrier = pltpu.get_barrier_semaphore()
    for peer in peers:
        pl.semaphore_signal(barrier, inc=1, device_id=(peer,), device_id_type=MESH)
    pl.semaphore_wait(barrier, len(peers))


def embed_kernel(x_img, x_txt, w_img, w_txt, e_img, e_txt):
    for x, w, e in ((x_img, w_img, e_img), (x_txt, w_txt, e_txt)):
        raw = jnp.dot(x[...], w[...], preferred_element_type=F32)
        inv = lax.rsqrt(jnp.sum(raw * raw, axis=1, keepdims=True))
        e[...] = (raw * inv).astype(BF16)


def embed(feat_img, feat_txt, w_img, w_txt):
    rows, blk = feat_img.shape[0], 512
    width = w_img.shape[1]
    by_row = lambda n: pl.BlockSpec((blk, n), lambda i: (i, 0))
    whole = lambda w: pl.BlockSpec(w.shape, lambda i: (0, 0))
    return pl.pallas_call(
        embed_kernel, name="embed", grid=(rows // blk,),
        out_shape=(jax.ShapeDtypeStruct((rows, width), BF16), jax.ShapeDtypeStruct((rows, width), BF16)),
        in_specs=[by_row(feat_img.shape[1]), by_row(feat_txt.shape[1]), whole(w_img), whole(w_txt)],
        out_specs=(by_row(width), by_row(width)),
    )(feat_img, feat_txt, w_img, w_txt)


def weight_kernel(scale, x_img, x_txt, w_img, w_txt, d_img, d_txt, sums, dw, part):
    first = pl.program_id(0) == 0
    n_img = x_img.shape[1]

    @pl.when(first)
    def _():
        dw[...] = jnp.zeros_like(dw)
        for k in range(4):
            total = sums[k, :, 0:128]
            for j in range(1, sums.shape[2] // 128):
                total = total + sums[k, :, j * 128:(j + 1) * 128]
            part[:, k * 128:(k + 1) * 128] = total

    for x, w, d, span in ((x_img, w_img, d_img, slice(0, n_img)), (x_txt, w_txt, d_txt, slice(n_img, dw.shape[0]))):
        raw = jnp.dot(x[...], w[...], preferred_element_type=F32)
        inv = lax.rsqrt(jnp.sum(raw * raw, axis=1, keepdims=True))
        unit = raw * inv
        grad = scale[0] * d[...]
        raw_grad = inv * (grad - unit * jnp.sum(unit * grad, axis=1, keepdims=True))
        dw[span, :] += lax.dot_general(x[...], raw_grad.astype(BF16), CONTRACT_ROWS, preferred_element_type=F32)


def weight_grads(scale, feat_img, feat_txt, w_img, w_txt, d_img, d_txt, sums):
    rows, blk = feat_img.shape[0], 512
    width = w_img.shape[1]
    n_all = feat_img.shape[1] + feat_txt.shape[1]
    by_row = lambda n: pl.BlockSpec((blk, n), lambda i: (i, 0))
    whole = lambda shape: pl.BlockSpec(shape, lambda i: (0,) * len(shape))
    return pl.pallas_call(
        weight_kernel, name="weight_grads", grid=(rows // blk,),
        out_shape=(jax.ShapeDtypeStruct((n_all, width), F32), jax.ShapeDtypeStruct((8, 512), F32)),
        in_specs=[pl.BlockSpec(memory_space=pltpu.SMEM), by_row(feat_img.shape[1]), by_row(feat_txt.shape[1]),
                  whole(w_img.shape), whole(w_txt.shape), by_row(width), by_row(width), whole(sums.shape)],
        out_specs=(whole((n_all, width)), whole((8, 512))),
    )(scale, feat_img, feat_txt, w_img, w_txt, d_img, d_txt, sums)


def reduce_kernel(x, part, out, total, acc, got, got_a, got_b, got_a2, got_b2, parts, send_sem, recv_sem, p_send, p_recv):
    me = lax.axis_index("data")
    core, cx, cy = me % 2, (me // 2) % 2, me // 4
    partner = flip_bits(core, cx, cy, 1, 0, 0)
    xn, yn = flip_bits(core, cx, cy, 0, 1, 0), flip_bits(core, cx, cy, 0, 0, 1)
    peers = [flip_bits(core, cx, cy, k % 2, (k // 2) % 2, k // 4) for k in range(1, 8)]
    enter(me, peers)
    half = x.shape[0] // 2
    quarter = half // 4
    eighth = quarter // 2

    def rows(start, size):
        return pl.ds(pl.multiple_of(start, 8), size)

    def copy(src, dst, k, to):
        return pltpu.make_async_remote_copy(src_ref=src, dst_ref=dst, send_sem=send_sem.at[k], recv_sem=recv_sem.at[k],
                                            device_id=(to,), device_id_type=MESH)

    def both(one, two):
        one.start()
        two.start()
        one.wait()
        two.wait()

    fold_halves = copy(x.at[rows((1 - core) * half, half)], got, 0, partner)
    fold_halves.start()
    part_copies = [
        pltpu.make_async_remote_copy(src_ref=part, dst_ref=parts.at[me], send_sem=p_send.at[k], recv_sem=p_recv.at[k],
                                     device_id=(peers[k],), device_id_type=MESH) for k in range(7)]
    for cp in part_copies:
        cp.start()
    parts[pl.ds(me, 1)] = part[...][None]
    fold_halves.wait()
    acc[...] = x[rows(core * half, half), :] + got[...]
    a1, b1 = cx * quarter, 2 * quarter + cy * quarter
    both(copy(acc.at[rows((1 - cx) * quarter, quarter)], got_a, 1, xn),
         copy(acc.at[rows(2 * quarter + (1 - cy) * quarter, quarter)], got_b, 2, yn))
    acc[rows(a1, quarter), :] += got_a[...]
    acc[rows(b1, quarter), :] += got_b[...]
    a2, b2 = a1 + cy * eighth, b1 + cx * eighth
    both(copy(acc.at[rows(a1 + (1 - cy) * eighth, eighth)], got_a2, 3, yn),
         copy(acc.at[rows(b1 + (1 - cx) * eighth, eighth)], got_b2, 4, xn))
    base = core * half
    out[rows(base + a2, eighth), :] = acc[rows(a2, eighth), :] + got_a2[...]
    out[rows(base + b2, eighth), :] = acc[rows(b2, eighth), :] + got_b2[...]

    def spread(start, size, k, to):
        span = rows(base + start, size)
        return copy(out.at[span], out.at[span], k, to)

    both(spread(a2, eighth, 5, yn), spread(b2, eighth, 6, xn))
    both(spread(a1, quarter, 7, xn), spread(b1, quarter, 8, yn))
    last = spread(0, half, 9, partner)
    last.start()
    for cp in part_copies:
        cp.wait()
    sum_parts = parts[0]
    for k in range(1, N_DEV):
        sum_parts = sum_parts + parts[k]
    total[...] = sum_parts
    last.wait()


def all_reduce(x, part):
    half, width = x.shape[0] // 2, x.shape[1]
    vmem = pl.BlockSpec(memory_space=pltpu.VMEM)
    buf = lambda n: pltpu.VMEM((n, width), F32)
    return pl.pallas_call(
        reduce_kernel, name="all_reduce",
        out_shape=(jax.ShapeDtypeStruct(x.shape, F32), jax.ShapeDtypeStruct(part.shape, F32)),
        in_specs=[vmem, vmem], out_specs=(vmem, vmem),
        scratch_shapes=[buf(half), buf(half), buf(half // 4), buf(half // 4), buf(half // 8), buf(half // 8),
                        pltpu.VMEM((N_DEV,) + part.shape, F32),
                        pltpu.SemaphoreType.DMA((10,)), pltpu.SemaphoreType.DMA((10,)),
                        pltpu.SemaphoreType.DMA((7,)), pltpu.SemaphoreType.DMA((7,))],
        compiler_params=pltpu.CompilerParams(collective_id=1, has_side_effects=True),
    )(x, part)


def pair_kernel(coef, emb_img, emb_txt, ids_row, ids_col, d_img, d_txt, sums,
                all_img, all_txt, all_ids, sb_img, sb_txt, gb_img, gb_txt, send_sem, recv_sem, id_send, id_recv, own_sem):
    me = lax.axis_index("data")
    core, cx, cy = me % 2, (me // 2) % 2, me // 4
    rows = emb_img.shape[0]
    half = rows // 2

    flip = functools.partial(flip_bits, core, cx, cy)
    flips = {REL_P: (1, 0, 0), REL_X: (0, 1, 0), REL_Y: (0, 0, 1), REL_XP: (1, 1, 0), REL_YP: (1, 0, 1),
             REL_D: (0, 1, 1), REL_DP: (1, 1, 1)}
    dev = {rel: flip(*bits) for rel, bits in flips.items()}

    enter(me, [dev[rel] for rel in range(7)])

    gathered = (all_txt, all_img)
    own = (emb_txt, emb_img)

    def copy_of(feat, hf, src_rel, to_rel, land_rel):
        span = pl.ds(hf * half, half)
        if src_rel is None:
            src, at = own[feat].at[span], me
        else:
            src, at = gathered[feat].at[dev[src_rel], span], dev[src_rel]
        return pltpu.make_async_remote_copy(
            src_ref=src, dst_ref=gathered[feat].at[at, span],
            send_sem=send_sem.at[feat, land_rel, hf], recv_sem=recv_sem.at[feat, land_rel, hf],
            device_id=(dev[to_rel],), device_id_type=MESH)

    T, I = 0, 1
    sends = []

    def send(feat, hf, src_rel, to_rel, land_rel):
        cp = copy_of(feat, hf, src_rel, to_rel, land_rel)
        cp.start()
        sends.append((feat, hf, src_rel, to_rel, land_rel))

    def arrive(feat, hf, rel):
        span = pl.ds(hf * half, half)
        pltpu.make_async_remote_copy(
            src_ref=own[feat].at[span], dst_ref=gathered[feat].at[dev[rel], span],
            send_sem=send_sem.at[feat, rel, hf], recv_sem=recv_sem.at[feat, rel, hf],
            device_id=(dev[REL_P],), device_id_type=MESH).wait_recv()

    id_copies = []
    for rel in range(7):
        cp = pltpu.make_async_remote_copy(
            src_ref=ids_col, dst_ref=all_ids.at[me], send_sem=id_send.at[rel], recv_sem=id_recv.at[rel],
            device_id=(dev[rel],), device_id_type=MESH)
        cp.start()
        id_copies.append(cp)
    for hf in range(2):
        send(T, hf, None, REL_X, REL_X)
        send(I, hf, None, REL_Y, REL_Y)
        send(I, hf, None, REL_X, REL_X)
        send(T, hf, None, REL_Y, REL_Y)
        send(T, hf, None, REL_P, REL_P)
        send(I, hf, None, REL_P, REL_P)
    locals_ = [pltpu.make_async_copy(emb_txt, all_txt.at[me], own_sem.at[0]),
               pltpu.make_async_copy(emb_img, all_img.at[me], own_sem.at[1]),
               pltpu.make_async_copy(ids_col, all_ids.at[me], own_sem.at[2])]
    for cp in locals_:
        cp.start()
    d_img[...] = jnp.zeros_like(d_img)
    d_txt[...] = jnp.zeros_like(d_txt)
    sums[...] = jnp.zeros_like(sums)
    for cp in locals_:
        cp.wait()

    a, b = coef[0], coef[1]
    n_row = rows // ROW_BLK
    n_col = rows // COL_BLK
    n_flat = N_DEV * n_col * n_row

    def where_at(step):
        g, q, e = step // 4, (step % 4) // 2, step % 2
        m0, m3, m2 = (3 - g) // 3, g // 3, (g % 3) // 2
        m12 = 1 - m0 - m3
        fc = m0 * q + (1 - m0) * e
        txt = flip(fc, m12 * (1 - q) + m3, m12 * q + m3)
        img = flip(fc, m12 * q + m3, m12 * (1 - q) + m3)
        return txt, m0 * e + m2 + m3 * (1 - q), img, m0 * e + m2 + m3 * q

    def scores(own_all, r0, other_all, at, hf):
        c0 = pl.multiple_of(hf * COL_BLK, COL_BLK)
        return lax.dot_general(own_all[me, pl.ds(r0, ROW_BLK), :], other_all[at, pl.ds(c0, COL_BLK), :], CONTRACT_COLS,
                               preferred_element_type=F32)

    def sign_of(r0, k, at, hf):
        ids_c = all_ids[at, :, pl.ds(pl.multiple_of(hf * COL_BLK, COL_BLK), COL_BLK)]
        ids_r = ids_row[pl.ds(r0 + k * STRIP, STRIP), 0:1]
        return jnp.where(ids_r == ids_c, -1.0, 1.0).astype(F32)

    def full_tile(r0, at, hf):
        run, low, gs_sum, g_sum = None, None, None, None
        for k in range(ROW_BLK // STRIP):
            s = sb_img[k * STRIP:(k + 1) * STRIP, :]
            sign = sign_of(r0, k, at, hf)
            neg = (s * a + b) * sign
            w = jnp.exp2(-jnp.abs(neg))
            d = 1.0 + w
            g = sign / (1.0 + jnp.exp2(neg))
            low_k, gs = jnp.minimum(neg, 0.0), g * s
            for u in range(STRIP // 8):
                at8 = slice(u * 8, u * 8 + 8)
                run = w[at8] if run is None else run * d[at8] + w[at8]
                low = low_k[at8] if low is None else low + low_k[at8]
                gs_sum = gs[at8] if gs_sum is None else gs_sum + gs[at8]
                g_sum = g[at8] if g_sum is None else g_sum + g[at8]
            gb_img[k * STRIP:(k + 1) * STRIP, :] = g.astype(BF16)
        sums[0] += low
        sums[1] += jnp.log1p(run)
        sums[2] += gs_sum
        sums[3] += g_sum

    def grad_tile(r0, at, hf):
        for k in range(ROW_BLK // STRIP):
            s = sb_txt[k * STRIP:(k + 1) * STRIP, :]
            sign = sign_of(r0, k, at, hf)
            gb_txt[k * STRIP:(k + 1) * STRIP, :] = (sign / (1.0 + jnp.exp2((s * a + b) * sign))).astype(BF16)

    sb_img[...] = scores(all_img, 0, all_txt, me, 0)

    @pl.loop(0, n_flat // n_row)
    def _(step):
        def on(s, arrivals, forwards=(), ids=False):
            @pl.when(step == s)
            def _():
                if ids:
                    for cp in id_copies:
                        cp.wait_recv()
                for item in arrivals:
                    arrive(*item)
                for item in forwards:
                    send(*item)

        on(1, [(T, 0, REL_P), (I, 0, REL_P)], ids=True)
        on(2, [(T, 1, REL_P), (I, 1, REL_P)])
        on(3, [(T, 0, REL_X), (I, 0, REL_Y)],
           [(T, 0, REL_X, REL_P, REL_XP), (I, 0, REL_Y, REL_P, REL_YP), (I, 0, REL_Y, REL_X, REL_D)])
        on(4, [(T, 0, REL_XP), (I, 0, REL_YP)])
        on(5, [(T, 0, REL_Y), (I, 0, REL_X)],
           [(T, 0, REL_Y, REL_P, REL_YP), (I, 0, REL_X, REL_P, REL_XP), (T, 0, REL_Y, REL_X, REL_D)])
        on(6, [(T, 0, REL_YP), (I, 0, REL_XP)])
        on(7, [(T, 1, REL_X), (I, 1, REL_Y)],
           [(T, 1, REL_X, REL_P, REL_XP), (I, 1, REL_Y, REL_P, REL_YP), (T, 1, REL_X, REL_Y, REL_D)])
        on(8, [(T, 1, REL_XP), (I, 1, REL_YP)])
        on(9, [(T, 1, REL_Y), (I, 1, REL_X)],
           [(T, 1, REL_Y, REL_P, REL_YP), (I, 1, REL_X, REL_P, REL_XP), (I, 1, REL_X, REL_Y, REL_D)])
        on(10, [(T, 1, REL_YP), (I, 1, REL_XP)])
        on(11, [(T, 1, REL_D), (I, 0, REL_D)], [(T, 1, REL_D, REL_P, REL_DP), (I, 0, REL_D, REL_P, REL_DP)])
        on(12, [(T, 1, REL_DP), (I, 0, REL_DP)])
        on(13, [(T, 0, REL_D), (I, 1, REL_D)], [(T, 0, REL_D, REL_P, REL_DP), (I, 1, REL_D, REL_P, REL_DP)])
        on(14, [(T, 0, REL_DP), (I, 1, REL_DP)])

        at_t, h_t, at_i, h_i = where_at(step)
        c_t = pl.multiple_of(h_t * COL_BLK, COL_BLK)
        c_i = pl.multiple_of(h_i * COL_BLK, COL_BLK)

        @pl.loop(0, n_row)
        def _(i):
            after = (step * n_row + i + 1) % n_flat
            at_n, h_n, _, _ = where_at(after // n_row)
            r0 = pl.multiple_of(i * ROW_BLK, ROW_BLK)
            r1 = pl.multiple_of((after % n_row) * ROW_BLK, ROW_BLK)
            tile = pl.ds(r0, ROW_BLK)
            sb_txt[...] = scores(all_txt, r0, all_img, at_i, h_i)
            full_tile(r0, at_t, h_t)
            d_img[tile, :] += jnp.dot(gb_img[...], all_txt[at_t, pl.ds(c_t, COL_BLK), :], preferred_element_type=F32)
            sb_img[...] = scores(all_img, r1, all_txt, at_n, h_n)
            grad_tile(r0, at_i, h_i)
            d_txt[tile, :] += jnp.dot(gb_txt[...], all_img[at_i, pl.ds(c_i, COL_BLK), :], preferred_element_type=F32)

    for cp in id_copies:
        cp.wait_send()
    for item in sends:
        copy_of(*item).wait_send()


def pair_grads(coef, emb_img, emb_txt, ids):
    rows, width = emb_img.shape
    vmem = pl.BlockSpec(memory_space=pltpu.VMEM)
    hbm = pl.BlockSpec(memory_space=pl.ANY)
    ids_row = jnp.broadcast_to(ids[:, None], (rows, 128))
    return pl.pallas_call(
        pair_kernel,
        name="pair_grads",
        out_shape=(jax.ShapeDtypeStruct((rows, width), F32), jax.ShapeDtypeStruct((rows, width), F32),
                   jax.ShapeDtypeStruct((4, 8, COL_BLK), F32)),
        in_specs=[pl.BlockSpec(memory_space=pltpu.SMEM), hbm, hbm, vmem, hbm],
        out_specs=(vmem, vmem, vmem),
        scratch_shapes=[
            pltpu.VMEM((N_DEV, rows, width), BF16),
            pltpu.VMEM((N_DEV, rows, width), BF16),
            pltpu.VMEM((N_DEV, 1, rows), jnp.int32),
            pltpu.VMEM((ROW_BLK, COL_BLK), F32),
            pltpu.VMEM((ROW_BLK, COL_BLK), F32),
            pltpu.VMEM((ROW_BLK, COL_BLK), BF16),
            pltpu.VMEM((ROW_BLK, COL_BLK), BF16),
            pltpu.SemaphoreType.DMA((2, 7, 2)),
            pltpu.SemaphoreType.DMA((2, 7, 2)),
            pltpu.SemaphoreType.DMA((7,)),
            pltpu.SemaphoreType.DMA((7,)),
            pltpu.SemaphoreType.DMA((3,)),
        ],
        compiler_params=pltpu.CompilerParams(collective_id=0, has_side_effects=True, vmem_limit_bytes=67_000_000),
    )(coef, emb_img, emb_txt, ids_row, ids[None, :])


def solution(mesh):
    n_dev = mesh.shape["data"]

    def local_fn(feat_img, feat_txt, w_img, w_txt, log_temp, logit_bias, pair_ids):
        total_rows = feat_img.shape[0] * n_dev
        temp_scale = jnp.exp(log_temp)
        emb_img, emb_txt = embed(feat_img, feat_txt, w_img, w_txt)
        coef = jnp.stack([-LOG2E * temp_scale, -LOG2E * logit_bias])
        d_img, d_txt, sums = pair_grads(coef, emb_img, emb_txt, pair_ids)
        scale = temp_scale / total_rows
        dw, part = weight_grads(scale[None], feat_img, feat_txt, w_img, w_txt, d_img, d_txt, sums)
        dw, total = all_reduce(dw, part)
        total = jnp.sum(total.reshape(8, 4, 128), axis=(0, 2))
        n_img = feat_img.shape[1]
        loss = (total[1] - total[0] / LOG2E) / total_rows
        return loss, scale * total[2], total[3] / total_rows, dw[:n_img], dw[n_img:]

    return jax.shard_map(
        local_fn,
        mesh=mesh,
        in_specs=(P("data", None), P("data", None), P(None, None), P(None, None), P(), P(), P("data")),
        out_specs=(P(), P(), P(), P(None, None), P(None, None)),
        check_vma=False,
    )
```

time: 956 us -> 301 us (0.31)
  waiting for transfers between devices: 458 us -> 0 us
  matrix products: 370 us -> 0 us
  Pallas kernels: 0 us -> 284 us
  local copies, waits for them, and re-layouts: 54.9 us -> 7.53 us
  blocking collectives: 22.8 us -> 0 us
  between operations: 21 us -> 7.97 us
  loops' own time: 13 us -> 0 us
    ppermute x22 -> x0, waiting for transfers between devices: 429 us -> none  [the longest x21 400 us: visit_block(): lax.ppermute((txt_blk, ids_blk, acc_txt + part_txt), 'data', next_perm)]
    dot_general x28 -> x0, matrix products: 370 us -> none  [the longest x8 194 us: tile_terms(): lax.dot_general(emb_img, emb_txt, CONTRACT_COLS, preferred_element_type=j...]
    pallas_call x0 -> x4, Pallas kernels: none -> 284 us  [the longest x1 227 us: pair_grads(): pl.pallas_call(pair_kernel, name='pair_grads', out_shape=(jax.ShapeDtypeS...]
    while x44 -> x0, local copies, waits for them, and re-layouts: 33.2 us -> none
    psum x1 -> x0, waiting for transfers between devices: 29.5 us -> none  [local_fn(): lax.psum((loss_sum + loss_part, temp_sum + temp_part, bias_sum + bias_par...]
    psum x1 -> x0, blocking collectives: 22.8 us -> none  [local_fn(): lax.psum((loss_sum + loss_part, temp_sum + temp_part, bias_sum + bias_par...]
    unnamed x33 -> x0, local copies, waits for them, and re-layouts: 19.2 us -> none
    another operation x1 -> x0, loops' own time: 13 us -> none  [local_fn(): loop_state = lax.fori_loop(0, n_dev - 1, visit_block, loop_state)]
  transfers between devices with their start and end apart: 23 -> 0, of which waited for: 9 -> 0; matrix products, arithmetic and copies ran while one was open for 10% -> 0% of each run, Pallas kernels for 0% -> 0%
where the time goes in v1:
time: 301 us
  Pallas kernels  284 us (94%)
  between operations  7.97 us (3%)
  local copies, waits for them, and re-layouts  7.53 us (3%)
    pallas_call x1, Pallas kernels, pair_grads(): pl.pallas_call(pair_kernel, name='pair_grads', out_shape=(jax.ShapeDtypeS...  227 us
    pallas_call x1, Pallas kernels, all_reduce(): pl.pallas_call(reduce_kernel, name='all_reduce', out_shape=(jax.ShapeDtyp...  37.1 us
    pallas_call x1, Pallas kernels, weight_grads(): pl.pallas_call(weight_kernel, name='weight_grads', grid=(rows // blk,), o...  13.2 us
    pallas_call x1, Pallas kernels, embed(): pl.pallas_call(embed_kernel, name='embed', grid=(rows // blk,), out_shape...  6.9 us

profile of v1, /device:TPU:0, one launch (start us, length us, event | category | flops | bytes accessed | tf_op | source)
XLA Modules:
  0.0 301.0 jit_solution(17853874136395571209)
XLA Ops:
  2.0 0.6 pad_maximum_fusion.coef
  2.5 2.0 broadcast_in_dim.13.ids_row
  4.6 6.9 %embed.1 = (bf16[2048,512]{1,0:T(8,128)(2,1)}, bf16[2048,512]{1,0:T(8,128)(2,1)}) custom-call(bf16[2048,768]{1,0:T(8,128)(2,1)} %x_img.3, bf16[2048,512]{1,0:T(8,128)(2,1)} %x_txt.3, bf16[768,512]{1,0:T(8,128)(2,1)} %w_img.3, bf16[512,512]{1,0:T(8,128)(2,1)} %w_txt.3), custom_call_target="tpu_custom_call" | custom-call | tf_op jit(solution)/shard_map/embed/pallas_call | solution.py:47
  11.5 226.8 %pair_grads.1 = (f32[2048,512]{1,0:T(8,128)}, f32[2048,512]{1,0:T(8,128)}, f32[4,8,1024]{2,1,0:T(8,128)}) custom-call(f32[2]{0:T(128)} %pad_maximum_fusion.coef, bf16[2048,512]{1,0:T(8,128)(2,1)} %get-tuple-element.14.emb_img, bf16[2048,512]{1,0:T(8,128)(2,1)} %get-tuple-element.15.emb_txt, s32[2048,128]{1,0:T(8,128)} %broadcast_in_dim.13.ids_row, ...), custom_call_target="tpu_custom_call" | custom-call | tf_op jit(solution)/shard_map/pair_grads/pallas_call | solution.py:354
  238.3 13.2 %weight_grads.1 = (f32[1280,512]{1,0:T(8,128)}, f32[8,512]{1,0:T(8,128)}) custom-call(f32[1]{0:T(128)} %bitcast.scale, bf16[2048,768]{1,0:T(8,128)(2,1)} %x_img.3, bf16[2048,512]{1,0:T(8,128)(2,1)} %x_txt.3, bf16[768,512]{1,0:T(8,128)(2,1)} %w_img.3, bf16[512,512]{1,0:T(8,128)(2,1)} %w_txt.3, f32[2048,512]{1,0:T(8,128)} %get-tuple-element.16.d_img, ...), custom_call_target="tpu_custom_call" | custom-call | tf_op jit(solution)/shard_map/weight_grads/pallas_call | solution.py:83
  251.5 37.1 %all_reduce.1 = (f32[1280,512]{1,0:T(8,128)}, f32[8,512]{1,0:T(8,128)}) custom-call(f32[1280,512]{1,0:T(8,128)} %get-tuple-element.19.x, f32[8,512]{1,0:T(8,128)} %get-tuple-element.20.part), custom_call_target="tpu_custom_call" | custom-call | tf_op jit(solution)/shard_map/all_reduce/pallas_call | solution.py:159
  288.6 0.7 reduce_sum.10
  289.3 0.1 bitcast_reduce_fusion
  289.5 0.6 fusion
  292.7 2.3 slice.23
  294.9 2.7 slice.22

commit v2 on v1

v2 whole, which is shorter than its diff:
```python
import functools

import jax
import jax.numpy as jnp
from jax import lax
from jax.experimental import pallas as pl
from jax.experimental.pallas import tpu as pltpu
from jax.sharding import PartitionSpec as P

CONTRACT_ROWS = (((0,), (0,)), ((), ()))
CONTRACT_COLS = (((1,), (1,)), ((), ()))
F32 = jnp.float32
BF16 = jnp.bfloat16
MESH = pl.DeviceIdType.MESH
LOG2E = 1.4426950408889634
N_DEV = 8
ROW_BLK = 512
COL_BLK = 1024
STRIP = 64


def flip_bits(core, cx, cy, fc, fx, fy):
    return (core + fc - 2 * core * fc) + 2 * (cx + fx - 2 * cx * fx) + 4 * (cy + fy - 2 * cy * fy)


def enter(me, peers):
    barrier = pltpu.get_barrier_semaphore()
    for peer in peers:
        pl.semaphore_signal(barrier, inc=1, device_id=(peer,), device_id_type=MESH)
    pl.semaphore_wait(barrier, len(peers))


def embed_kernel(x_img, x_txt, w_img, w_txt, e_img, e_txt):
    for x, w, e in ((x_img, w_img, e_img), (x_txt, w_txt, e_txt)):
        raw = jnp.dot(x[...], w[...], preferred_element_type=F32)
        inv = lax.rsqrt(jnp.sum(raw * raw, axis=1, keepdims=True))
        e[...] = (raw * inv).astype(BF16)


def embed(feat_img, feat_txt, w_img, w_txt):
    rows, blk = feat_img.shape[0], 512
    width = w_img.shape[1]
    by_row = lambda n: pl.BlockSpec((blk, n), lambda i: (i, 0))
    whole = lambda w: pl.BlockSpec(w.shape, lambda i: (0, 0))
    return pl.pallas_call(
        embed_kernel, name="embed", grid=(rows // blk,),
        out_shape=(jax.ShapeDtypeStruct((rows, width), BF16), jax.ShapeDtypeStruct((rows, width), BF16)),
        in_specs=[by_row(feat_img.shape[1]), by_row(feat_txt.shape[1]), whole(w_img), whole(w_txt)],
        out_specs=(by_row(width), by_row(width)),
    )(feat_img, feat_txt, w_img, w_txt)


def weight_kernel(scale, x_img, x_txt, w_img, w_txt, d_img, r_x, d_txt, r_p, r_y, sums, dw, part):
    first = pl.program_id(0) == 0
    n_img = x_img.shape[1]

    @pl.when(first)
    def _():
        dw[...] = jnp.zeros_like(dw)
        for k in range(4):
            total = sums[k, :, 0:128]
            for j in range(1, sums.shape[2] // 128):
                total = total + sums[k, :, j * 128:(j + 1) * 128]
            part[:, k * 128:(k + 1) * 128] = total

    for x, w, terms, span in ((x_img, w_img, (d_img, r_x), slice(0, n_img)),
                              (x_txt, w_txt, (d_txt, r_p, r_y), slice(n_img, dw.shape[0]))):
        raw = jnp.dot(x[...], w[...], preferred_element_type=F32)
        inv = lax.rsqrt(jnp.sum(raw * raw, axis=1, keepdims=True))
        unit = raw * inv
        total = terms[0][...]
        for term in terms[1:]:
            total = total + term[...]
        grad = scale[0] * total
        raw_grad = inv * (grad - unit * jnp.sum(unit * grad, axis=1, keepdims=True))
        dw[span, :] += lax.dot_general(x[...], raw_grad.astype(BF16), CONTRACT_ROWS, preferred_element_type=F32)


def weight_grads(scale, feat_img, feat_txt, w_img, w_txt, terms, sums):
    rows, blk = feat_img.shape[0], 512
    width = w_img.shape[1]
    n_all = feat_img.shape[1] + feat_txt.shape[1]
    by_row = lambda n: pl.BlockSpec((blk, n), lambda i: (i, 0))
    whole = lambda shape: pl.BlockSpec(shape, lambda i: (0,) * len(shape))
    return pl.pallas_call(
        weight_kernel, name="weight_grads", grid=(rows // blk,),
        out_shape=(jax.ShapeDtypeStruct((n_all, width), F32), jax.ShapeDtypeStruct((8, 512), F32)),
        in_specs=[pl.BlockSpec(memory_space=pltpu.SMEM), by_row(feat_img.shape[1]), by_row(feat_txt.shape[1]),
                  whole(w_img.shape), whole(w_txt.shape), *[by_row(width)] * len(terms), whole(sums.shape)],
        out_specs=(whole((n_all, width)), whole((8, 512))),
    )(scale, feat_img, feat_txt, w_img, w_txt, *terms, sums)


def reduce_kernel(x, part, out, total, acc, got, got_a, got_b, got_a2, got_b2, parts, send_sem, recv_sem, p_send, p_recv):
    me = lax.axis_index("data")
    core, cx, cy = me % 2, (me // 2) % 2, me // 4
    partner = flip_bits(core, cx, cy, 1, 0, 0)
    xn, yn = flip_bits(core, cx, cy, 0, 1, 0), flip_bits(core, cx, cy, 0, 0, 1)
    peers = [flip_bits(core, cx, cy, k % 2, (k // 2) % 2, k // 4) for k in range(1, 8)]
    enter(me, peers)
    half = x.shape[0] // 2
    quarter = half // 4
    eighth = quarter // 2

    def rows(start, size):
        return pl.ds(pl.multiple_of(start, 8), size)

    def copy(src, dst, k, to):
        return pltpu.make_async_remote_copy(src_ref=src, dst_ref=dst, send_sem=send_sem.at[k], recv_sem=recv_sem.at[k],
                                            device_id=(to,), device_id_type=MESH)

    def both(one, two):
        one.start()
        two.start()
        one.wait()
        two.wait()

    fold_halves = copy(x.at[rows((1 - core) * half, half)], got, 0, partner)
    fold_halves.start()
    part_copies = [
        pltpu.make_async_remote_copy(src_ref=part, dst_ref=parts.at[me], send_sem=p_send.at[k], recv_sem=p_recv.at[k],
                                     device_id=(peers[k],), device_id_type=MESH) for k in range(7)]
    for cp in part_copies:
        cp.start()
    parts[pl.ds(me, 1)] = part[...][None]
    fold_halves.wait()
    acc[...] = x[rows(core * half, half), :] + got[...]
    a1, b1 = cx * quarter, 2 * quarter + cy * quarter
    both(copy(acc.at[rows((1 - cx) * quarter, quarter)], got_a, 1, xn),
         copy(acc.at[rows(2 * quarter + (1 - cy) * quarter, quarter)], got_b, 2, yn))
    acc[rows(a1, quarter), :] += got_a[...]
    acc[rows(b1, quarter), :] += got_b[...]
    a2, b2 = a1 + cy * eighth, b1 + cx * eighth
    both(copy(acc.at[rows(a1 + (1 - cy) * eighth, eighth)], got_a2, 3, yn),
         copy(acc.at[rows(b1 + (1 - cx) * eighth, eighth)], got_b2, 4, xn))
    base = core * half
    out[rows(base + a2, eighth), :] = acc[rows(a2, eighth), :] + got_a2[...]
    out[rows(base + b2, eighth), :] = acc[rows(b2, eighth), :] + got_b2[...]

    def spread(start, size, k, to):
        span = rows(base + start, size)
        return copy(out.at[span], out.at[span], k, to)

    both(spread(a2, eighth, 5, yn), spread(b2, eighth, 6, xn))
    both(spread(a1, quarter, 7, xn), spread(b1, quarter, 8, yn))
    last = spread(0, half, 9, partner)
    last.start()
    for cp in part_copies:
        cp.wait()
    sum_parts = parts[0]
    for k in range(1, N_DEV):
        sum_parts = sum_parts + parts[k]
    total[...] = sum_parts
    last.wait()


def all_reduce(x, part):
    half, width = x.shape[0] // 2, x.shape[1]
    vmem = pl.BlockSpec(memory_space=pltpu.VMEM)
    buf = lambda n: pltpu.VMEM((n, width), F32)
    return pl.pallas_call(
        reduce_kernel, name="all_reduce",
        out_shape=(jax.ShapeDtypeStruct(x.shape, F32), jax.ShapeDtypeStruct(part.shape, F32)),
        in_specs=[vmem, vmem], out_specs=(vmem, vmem),
        scratch_shapes=[buf(half), buf(half), buf(half // 4), buf(half // 4), buf(half // 8), buf(half // 8),
                        pltpu.VMEM((N_DEV,) + part.shape, F32),
                        pltpu.SemaphoreType.DMA((10,)), pltpu.SemaphoreType.DMA((10,)),
                        pltpu.SemaphoreType.DMA((7,)), pltpu.SemaphoreType.DMA((7,))],
        compiler_params=pltpu.CompilerParams(collective_id=1, has_side_effects=True),
    )(x, part)


def tile_at(t):
    def from_(s, n):
        return lax.div(n + 64 - s, 64)

    early = 1 - from_(16, t)
    late = t + 16 * early
    b1, b2, b3 = from_(31, late), from_(44, late), from_(55, late)
    k = b1 + b2 + b3
    u = late - (16 + 15 * b1 + 13 * b2 + 11 * b3)
    v = u - (8 - k)
    is_col = from_(0, v)
    i = (1 - is_col) * (4 + k) + is_col * (v + (k + 1) * from_(4, v))
    j = (1 - is_col) * (u + k * from_(4, u)) + is_col * (4 + k)
    return early * lax.rem(t, 4) + (1 - early) * i, early * lax.div(t, 4) + (1 - early) * j


def pair_kernel(coef, emb_img, emb_txt, ids_sq, ids_half, ids_quarter, d_img, d_txt, r_x, r_p, r_y, sums,
                img, txt, di, dt, comb, ids_row, ids_col, ids_x, sb0, sb1, gb0, gb1, send_sem, recv_sem, own_sem):
    me = lax.axis_index("data")
    core, cx, cy = me % 2, (me // 2) % 2, me // 4
    flip = functools.partial(flip_bits, core, cx, cy)
    partner, xn, yn, yp = flip(1, 0, 0), flip(0, 1, 0), flip(0, 0, 1), flip(1, 0, 1)
    rows = emb_img.shape[0]
    q_rows = rows // 4
    enter(me, [partner, xn, yn, yp])

    def copy(k, src, dst, to):
        return pltpu.make_async_remote_copy(src_ref=src, dst_ref=dst, send_sem=send_sem.at[k], recv_sem=recv_sem.at[k],
                                            device_id=(to,), device_id_type=MESH)

    low, high = pl.ds(0, q_rows), pl.ds(q_rows, q_rows)

    def quarter(q):
        return pl.ds(q * q_rows, q_rows)

    feat_x = [copy(q, emb_img.at[quarter(q)], img.at[pl.ds(rows + q * q_rows, q_rows)], xn) for q in range(4)]
    feat_y = [copy(4 + q, emb_txt.at[quarter(q)], txt.at[4 + q, low], yn) for q in range(4)]
    feat_p = [copy(8 + h, emb_txt.at[pl.ds(h * COL_BLK, COL_BLK)], txt.at[2 + h], partner) for h in range(2)]
    pass_p = [copy(10 + q, txt.at[4 + q, low], txt.at[4 + q, high], partner) for q in range(4)]
    part_x = [copy(14 + q, di.at[pl.ds(rows + q * q_rows, q_rows)], r_x.at[quarter(q)], xn) for q in range(4)]
    part_c = [copy(18 + q, dt.at[4 + q, high], comb.at[q], partner) for q in range(4)]
    part_y = [copy(22 + q, dt.at[4 + q, low], r_y.at[quarter(q)], yn) for q in range(4)]
    part_p = [copy(26 + h, dt.at[2 + h], r_p.at[pl.ds(h * COL_BLK, COL_BLK)], partner) for h in range(2)]
    ids_p = copy(28, ids_half, ids_col.at[pl.ds(2, 2)], partner)
    ids_y = copy(29, ids_quarter, ids_col.at[pl.ds(4, 4), :, low], yn)
    ids_yp = copy(30, ids_quarter, ids_col.at[pl.ds(4, 4), :, high], yp)
    ids_xn = copy(31, ids_sq, ids_x.at[1], xn)
    every = [*feat_x, *feat_y, *feat_p, *pass_p, *part_x, *part_c, *part_y, *part_p, ids_p, ids_y, ids_yp, ids_xn]

    for cp in (ids_xn, ids_p, ids_y, ids_yp):
        cp.start()
    for q in range(4):
        feat_x[q].start()
        feat_y[q].start()
    for cp in feat_p:
        cp.start()
    own = [pltpu.make_async_copy(emb_img, img.at[pl.ds(0, rows)], own_sem.at[0]),
           pltpu.make_async_copy(emb_txt.at[pl.ds(0, COL_BLK)], txt.at[0], own_sem.at[1]),
           pltpu.make_async_copy(emb_txt.at[pl.ds(COL_BLK, COL_BLK)], txt.at[1], own_sem.at[2]),
           pltpu.make_async_copy(ids_half, ids_col.at[pl.ds(0, 2)], own_sem.at[3]),
           pltpu.make_async_copy(ids_sq, ids_x.at[0], own_sem.at[4])]
    for cp in own:
        cp.start()

    @pl.loop(0, 8)
    def _(k):
        di[pl.ds(pl.multiple_of(k * ROW_BLK, ROW_BLK), ROW_BLK), :] = jnp.zeros((ROW_BLK, di.shape[1]), F32)
        dt[k] = jnp.zeros(dt.shape[1:], F32)

    sums[...] = jnp.zeros_like(sums)
    gb1[...] = jnp.zeros_like(gb1)
    for cp in own:
        cp.wait()

    def spread_ids(which):
        columns = ids_x[which].T
        for k in range(rows // 128):
            ids_row[which * rows + k * 128:which * rows + (k + 1) * 128, :] = jnp.broadcast_to(
                columns[:, k:k + 1], (128, 128))

    spread_ids(0)
    a, b = coef[0], coef[1]
    n_tiles = 64

    def row_span(i):
        return pl.ds(pl.multiple_of(i * ROW_BLK, ROW_BLK), ROW_BLK)

    def scores(sb, t):
        i, j = tile_at(t)
        sb[...] = lax.dot_general(img[row_span(i), :], txt[j], CONTRACT_COLS, preferred_element_type=F32)

    def gradients(gb, t):
        i, j = tile_at(t)
        di[row_span(i), :] += jnp.dot(gb[...], txt[j], preferred_element_type=F32)
        dt[j] += lax.dot_general(gb[...], img[row_span(i), :], CONTRACT_ROWS, preferred_element_type=F32)

    def elementwise(sb, gb, t):
        i, j = tile_at(t)
        ids_c = ids_col[j]
        run, low_sum, gs_sum, g_sum = None, None, None, None
        for k in range(ROW_BLK // STRIP):
            s = sb[k * STRIP:(k + 1) * STRIP, :]
            ids_r = ids_row[pl.ds(i * ROW_BLK + k * STRIP, STRIP), 0:1]
            sign = jnp.where(ids_r == ids_c, -1.0, 1.0).astype(F32)
            neg = (s * a + b) * sign
            w = jnp.exp2(-jnp.abs(neg))
            d = 1.0 + w
            g = sign / (1.0 + jnp.exp2(neg))
            low_k, gs = jnp.minimum(neg, 0.0), g * s
            for u in range(STRIP // 8):
                at8 = slice(u * 8, u * 8 + 8)
                run = w[at8] if run is None else run * d[at8] + w[at8]
                low_sum = low_k[at8] if low_sum is None else low_sum + low_k[at8]
                gs_sum = gs[at8] if gs_sum is None else gs_sum + gs[at8]
                g_sum = g[at8] if g_sum is None else g_sum + g[at8]
            gb[k * STRIP:(k + 1) * STRIP, :] = g.astype(BF16)
        sums[0] += low_sum
        sums[1] += jnp.log1p(run)
        sums[2] += gs_sum
        sums[3] += g_sum

    def join(q):
        part_c[q].wait_recv()
        dt[4 + q, 0:q_rows, :] += comb[q]
        part_y[q].start()

    scores(sb0, 0)

    @pl.loop(0, n_tiles // 2)
    def _(f):
        def on(at, arrivals=(), starts=(), then=None):
            @pl.when(f == at)
            def _():
                for cp in arrivals:
                    cp.wait_recv()
                for cp in starts:
                    cp.start()
                if then is not None:
                    then()

        on(3, [*feat_p, ids_p])
        on(7, [feat_x[0], feat_y[0], feat_y[1], ids_y, ids_yp, ids_xn], [pass_p[0], pass_p[1]],
           then=functools.partial(spread_ids, 1))
        on(9, [pass_p[0], pass_p[1], feat_y[2]], [pass_p[2]])
        on(10, [pass_p[2], feat_y[3]], [pass_p[3]])
        on(11, [pass_p[3]])
        on(13, feat_x[1:], [part_x[0]])
        on(16, (), [part_c[0]])
        on(17, then=functools.partial(join, 0))
        on(20, (), [part_x[1]])
        on(23, (), [part_c[1]])
        on(24, then=functools.partial(join, 1))
        on(26, (), [part_x[2]])
        on(28, (), [part_c[2]])
        on(29, then=functools.partial(join, 2))
        on(31, (), [part_x[3], *part_p])

        t = 2 * f
        scores(sb1, t + 1)
        elementwise(sb0, gb0, t)
        gradients(gb1, jnp.maximum(t - 1, 0))
        scores(sb0, lax.rem(t + 2, n_tiles))
        elementwise(sb1, gb1, t + 1)
        gradients(gb0, t)

    gradients(gb1, n_tiles - 1)
    part_c[3].start()
    outs = [pltpu.make_async_copy(di.at[pl.ds(0, rows)], d_img, own_sem.at[0]),
            pltpu.make_async_copy(dt.at[0], d_txt.at[pl.ds(0, COL_BLK)], own_sem.at[1]),
            pltpu.make_async_copy(dt.at[1], d_txt.at[pl.ds(COL_BLK, COL_BLK)], own_sem.at[2])]
    for cp in outs:
        cp.start()
    join(3)
    for cp in outs:
        cp.wait()
    for cp in (*part_x, *part_p, *part_y):
        cp.wait_recv()
    for cp in every:
        cp.wait_send()


def pair_grads(coef, emb_img, emb_txt, ids):
    rows, width = emb_img.shape
    hbm = pl.BlockSpec(memory_space=pl.ANY)
    vmem = pl.BlockSpec(memory_space=pltpu.VMEM)
    grads = jax.ShapeDtypeStruct((rows, width), F32)
    return pl.pallas_call(
        pair_kernel,
        name="pair_grads",
        out_shape=(grads, grads, grads, grads, grads, jax.ShapeDtypeStruct((4, 8, COL_BLK), F32)),
        in_specs=[pl.BlockSpec(memory_space=pltpu.SMEM), hbm, hbm, hbm, hbm, hbm],
        out_specs=(hbm, hbm, hbm, hbm, hbm, vmem),
        scratch_shapes=[
            pltpu.VMEM((2 * rows, width), BF16),
            pltpu.VMEM((8, COL_BLK, width), BF16),
            pltpu.VMEM((2 * rows, width), F32),
            pltpu.VMEM((8, COL_BLK, width), F32),
            pltpu.VMEM((4, rows // 4, width), F32),
            pltpu.VMEM((2 * rows, 128), jnp.int32),
            pltpu.VMEM((8, 1, COL_BLK), jnp.int32),
            pltpu.VMEM((2, rows // 128, 128), jnp.int32),
            pltpu.VMEM((ROW_BLK, COL_BLK), F32),
            pltpu.VMEM((ROW_BLK, COL_BLK), F32),
            pltpu.VMEM((ROW_BLK, COL_BLK), BF16),
            pltpu.VMEM((ROW_BLK, COL_BLK), BF16),
            pltpu.SemaphoreType.DMA((32,)),
            pltpu.SemaphoreType.DMA((32,)),
            pltpu.SemaphoreType.DMA((5,)),
        ],
        compiler_params=pltpu.CompilerParams(collective_id=0, has_side_effects=True, vmem_limit_bytes=67_000_000),
    )(coef, emb_img, emb_txt, ids.reshape(rows // 128, 128), ids.reshape(2, 1, COL_BLK), ids.reshape(4, 1, rows // 4))


def solution(mesh):
    n_dev = mesh.shape["data"]

    def local_fn(feat_img, feat_txt, w_img, w_txt, log_temp, logit_bias, pair_ids):
        total_rows = feat_img.shape[0] * n_dev
        temp_scale = jnp.exp(log_temp)
        emb_img, emb_txt = embed(feat_img, feat_txt, w_img, w_txt)
        coef = jnp.stack([-LOG2E * temp_scale, -LOG2E * logit_bias])
        d_img, d_txt, r_x, r_p, r_y, sums = pair_grads(coef, emb_img, emb_txt, pair_ids)
        scale = temp_scale / total_rows
        dw, part = weight_grads(scale[None], feat_img, feat_txt, w_img, w_txt, (d_img, r_x, d_txt, r_p, r_y), sums)
        dw, total = all_reduce(dw, part)
        total = jnp.sum(total.reshape(8, 4, 128), axis=(0, 2))
        n_img = feat_img.shape[1]
        loss = (total[1] - total[0] / LOG2E) / total_rows
        return loss, scale * total[2], total[3] / total_rows, dw[:n_img], dw[n_img:]

    return jax.shard_map(
        local_fn,
        mesh=mesh,
        in_specs=(P("data", None), P("data", None), P(None, None), P(None, None), P(), P(), P("data")),
        out_specs=(P(), P(), P(), P(None, None), P(None, None)),
        check_vma=False,
    )
```

time: 301 us -> 310 us (1.030)
  Pallas kernels: 284 us -> 295 us
    pallas_call x1, Pallas kernels: 227 us -> 235 us  [pair_grads(): pl.pallas_call(pair_kernel, name='pair_grads', out_shape=(grads, grads, g...]
where the time goes in v2:
time: 310 us
  Pallas kernels  295 us (95%)
  between operations  7.97 us (3%)
  local copies, waits for them, and re-layouts  5.53 us (2%)
    pallas_call x1, Pallas kernels, pair_grads(): pl.pallas_call(pair_kernel, name='pair_grads', out_shape=(grads, grads, g...  235 us
    pallas_call x1, Pallas kernels, all_reduce(): pl.pallas_call(reduce_kernel, name='all_reduce', out_shape=(jax.ShapeDtyp...  37.8 us
    pallas_call x1, Pallas kernels, weight_grads(): pl.pallas_call(weight_kernel, name='weight_grads', grid=(rows // blk,), o...  15.4 us
    pallas_call x1, Pallas kernels, embed(): pl.pallas_call(embed_kernel, name='embed', grid=(rows // blk,), out_shape...  6.9 us

profile of v2, /device:TPU:0, one launch (start us, length us, event | category | flops | bytes accessed | tf_op | source)
XLA Modules:
  0.0 309.7 jit_solution(1706385022125106744)
XLA Ops:
  2.0 0.6 pad_maximum_fusion.coef
  2.5 6.9 %embed.1 = (bf16[2048,512]{1,0:T(8,128)(2,1)}, bf16[2048,512]{1,0:T(8,128)(2,1)}) custom-call(bf16[2048,768]{1,0:T(8,128)(2,1)} %x_img.3, bf16[2048,512]{1,0:T(8,128)(2,1)} %x_txt.3, bf16[768,512]{1,0:T(8,128)(2,1)} %w_img.3, bf16[512,512]{1,0:T(8,128)(2,1)} %w_txt.3), custom_call_target="tpu_custom_call" | custom-call | tf_op jit(solution)/shard_map/embed/pallas_call | solution.py:45
  9.5 234.7 %pair_grads.1 = (f32[2048,512]{1,0:T(8,128)}, f32[2048,512]{1,0:T(8,128)}, f32[2048,512]{1,0:T(8,128)}, f32[2048,512]{1,0:T(8,128)}, f32[2048,512]{1,0:T(8,128)}, /*index=5*/f32[4,8,1024]{2,1,0:T(8,128)}) custom-call(f32[2]{0:T(128)} %pad_maximum_fusion.coef, bf16[2048,512]{1,0:T(8,128)(2,1)} %get-tuple-element.17.emb_img, ...), custom_call_target="tpu_custom_call" | custom-call | tf_op jit(solution)/shard_map/pair_grads/pallas_call | solution.py:359
  244.1 15.4 %weight_grads.1 = (f32[1280,512]{1,0:T(8,128)}, f32[8,512]{1,0:T(8,128)}) custom-call(f32[1]{0:T(128)} %bitcast.scale, bf16[2048,768]{1,0:T(8,128)(2,1)} %x_img.3, bf16[2048,512]{1,0:T(8,128)(2,1)} %x_txt.3, bf16[768,512]{1,0:T(8,128)(2,1)} %w_img.3, bf16[512,512]{1,0:T(8,128)(2,1)} %w_txt.3, f32[2048,512]{1,0:T(8,128)} %get-tuple-element.19.d_img, ...), custom_call_target="tpu_custom_call" | custom-call | tf_op jit(solution)/shard_map/weight_grads/pallas_call | solution.py:85
  259.6 37.8 %all_reduce.1 = (f32[1280,512]{1,0:T(8,128)}, f32[8,512]{1,0:T(8,128)}) custom-call(f32[1280,512]{1,0:T(8,128)} %get-tuple-element.25.x, f32[8,512]{1,0:T(8,128)} %get-tuple-element.26.part), custom_call_target="tpu_custom_call" | custom-call | tf_op jit(solution)/shard_map/all_reduce/pallas_call | solution.py:161
  297.4 0.7 reduce_sum.10
  298.1 0.1 bitcast_reduce_fusion
  298.2 0.6 fusion
  301.4 2.3 slice.23
  303.7 2.7 slice.22

commit v3 on v2

--- a/solution.py
+++ b/solution.py
@@ -63,15 +63,12 @@
                 total = total + sums[k, :, j * 128:(j + 1) * 128]
             part[:, k * 128:(k + 1) * 128] = total
 
-    for x, w, terms, span in ((x_img, w_img, (d_img, r_x), slice(0, n_img)),
-                              (x_txt, w_txt, (d_txt, r_p, r_y), slice(n_img, dw.shape[0]))):
+    for x, w, terms, span in ((x_img, w_img, lambda: d_img[...] + r_x[...], slice(0, n_img)),
+                              (x_txt, w_txt, lambda: (d_txt[...] + r_p[...] + r_y[...]).T, slice(n_img, dw.shape[0]))):
         raw = jnp.dot(x[...], w[...], preferred_element_type=F32)
         inv = lax.rsqrt(jnp.sum(raw * raw, axis=1, keepdims=True))
         unit = raw * inv
-        total = terms[0][...]
-        for term in terms[1:]:
-            total = total + term[...]
-        grad = scale[0] * total
+        grad = scale[0] * terms()
         raw_grad = inv * (grad - unit * jnp.sum(unit * grad, axis=1, keepdims=True))
         dw[span, :] += lax.dot_general(x[...], raw_grad.astype(BF16), CONTRACT_ROWS, preferred_element_type=F32)
 
@@ -81,12 +78,13 @@
     width = w_img.shape[1]
     n_all = feat_img.shape[1] + feat_txt.shape[1]
     by_row = lambda n: pl.BlockSpec((blk, n), lambda i: (i, 0))
+    by_column = pl.BlockSpec((width, blk), lambda i: (0, i))
     whole = lambda shape: pl.BlockSpec(shape, lambda i: (0,) * len(shape))
     return pl.pallas_call(
         weight_kernel, name="weight_grads", grid=(rows // blk,),
         out_shape=(jax.ShapeDtypeStruct((n_all, width), F32), jax.ShapeDtypeStruct((8, 512), F32)),
         in_specs=[pl.BlockSpec(memory_space=pltpu.SMEM), by_row(feat_img.shape[1]), by_row(feat_txt.shape[1]),
-                  whole(w_img.shape), whole(w_txt.shape), *[by_row(width)] * len(terms), whole(sums.shape)],
+                  whole(w_img.shape), whole(w_txt.shape), by_row(width), by_row(width), *[by_column] * 3, whole(sums.shape)],
         out_specs=(whole((n_all, width)), whole((8, 512))),
     )(scale, feat_img, feat_txt, w_img, w_txt, *terms, sums)
 
@@ -170,24 +168,25 @@
     )(x, part)
 
 
+SEGMENTS = ((0, 0, 1, 0, 0), (4, 0, 1, 2, 0), (8, 4, 0, 0, 1), (12, 0, 1, 4, 0), (16, 5, 0, 0, 1), (20, 4, 1, 4, 0),
+            (24, 4, 0, 5, 1), (27, 5, 0, 5, 1), (30, 0, 1, 5, 0), (34, 6, 1, 5, 0), (36, 0, 1, 6, 0), (40, 6, 1, 6, 0),
+            (42, 6, 0, 0, 1), (46, 6, 0, 7, 0), (47, 7, 0, 0, 1), (51, 7, 0, 7, 0), (52, 0, 1, 7, 0), (56, 0, 1, 3, 0),
+            (60, 0, 1, 1, 0))
+
+
 def tile_at(t):
-    def from_(s, n):
-        return lax.div(n + 64 - s, 64)
-
-    early = 1 - from_(16, t)
-    late = t + 16 * early
-    b1, b2, b3 = from_(31, late), from_(44, late), from_(55, late)
-    k = b1 + b2 + b3
-    u = late - (16 + 15 * b1 + 13 * b2 + 11 * b3)
-    v = u - (8 - k)
-    is_col = from_(0, v)
-    i = (1 - is_col) * (4 + k) + is_col * (v + (k + 1) * from_(4, v))
-    j = (1 - is_col) * (u + k * from_(4, u)) + is_col * (4 + k)
-    return early * lax.rem(t, 4) + (1 - early) * i, early * lax.div(t, 4) + (1 - early) * j
+    code, last = 0, (0, 0)
+    for first, i, di, j, dj in SEGMENTS:
+        slope = 8 * di + dj
+        line = (8 * i + j - slope * first, slope)
+        step = (line[0] - last[0]) + (line[1] - last[1]) * t
+        code = code + (step if first == 0 else lax.div(t + (64 - first), 64) * step)
+        last = line
+    return lax.div(code, 8), lax.rem(code, 8)
 
 
 def pair_kernel(coef, emb_img, emb_txt, ids_sq, ids_half, ids_quarter, d_img, d_txt, r_x, r_p, r_y, sums,
-                img, txt, di, dt, comb, ids_row, ids_col, ids_x, sb0, sb1, gb0, gb1, send_sem, recv_sem, own_sem):
+                img, img_t, txt, di, dt, comb, ids_row, ids_col, ids_x, sb0, sb1, gb0, gb1, send_sem, recv_sem, own_sem):
     me = lax.axis_index("data")
     core, cx, cy = me % 2, (me // 2) % 2, me // 4
     flip = functools.partial(flip_bits, core, cx, cy)
@@ -210,9 +209,9 @@
     feat_p = [copy(8 + h, emb_txt.at[pl.ds(h * COL_BLK, COL_BLK)], txt.at[2 + h], partner) for h in range(2)]
     pass_p = [copy(10 + q, txt.at[4 + q, low], txt.at[4 + q, high], partner) for q in range(4)]
     part_x = [copy(14 + q, di.at[pl.ds(rows + q * q_rows, q_rows)], r_x.at[quarter(q)], xn) for q in range(4)]
-    part_c = [copy(18 + q, dt.at[4 + q, high], comb.at[q], partner) for q in range(4)]
-    part_y = [copy(22 + q, dt.at[4 + q, low], r_y.at[quarter(q)], yn) for q in range(4)]
-    part_p = [copy(26 + h, dt.at[2 + h], r_p.at[pl.ds(h * COL_BLK, COL_BLK)], partner) for h in range(2)]
+    part_c = [copy(18 + q, dt.at[4 + q, :, high], comb.at[q], partner) for q in range(4)]
+    part_y = [copy(22 + q, dt.at[4 + q, :, low], r_y.at[:, quarter(q)], yn) for q in range(4)]
+    part_p = [copy(26 + h, dt.at[2 + h], r_p.at[:, pl.ds(h * COL_BLK, COL_BLK)], partner) for h in range(2)]
     ids_p = copy(28, ids_half, ids_col.at[pl.ds(2, 2)], partner)
     ids_y = copy(29, ids_quarter, ids_col.at[pl.ds(4, 4), :, low], yn)
     ids_yp = copy(30, ids_quarter, ids_col.at[pl.ds(4, 4), :, high], yp)
@@ -250,7 +249,13 @@
             ids_row[which * rows + k * 128:which * rows + (k + 1) * 128, :] = jnp.broadcast_to(
                 columns[:, k:k + 1], (128, 128))
 
+    def flip_rows(first, count):
+        @pl.loop(first, first + count)
+        def _(i):
+            img_t[i] = img[pl.ds(pl.multiple_of(i * ROW_BLK, ROW_BLK), ROW_BLK), :].T
+
     spread_ids(0)
+    flip_rows(0, 4)
     a, b = coef[0], coef[1]
     n_tiles = 64
 
@@ -264,7 +269,7 @@
     def gradients(gb, t):
         i, j = tile_at(t)
         di[row_span(i), :] += jnp.dot(gb[...], txt[j], preferred_element_type=F32)
-        dt[j] += lax.dot_general(gb[...], img[row_span(i), :], CONTRACT_ROWS, preferred_element_type=F32)
+        dt[j] += jnp.dot(img_t[i], gb[...], preferred_element_type=F32)
 
     def elementwise(sb, gb, t):
         i, j = tile_at(t)
@@ -293,8 +298,12 @@
 
     def join(q):
         part_c[q].wait_recv()
-        dt[4 + q, 0:q_rows, :] += comb[q]
+        dt[4 + q, :, 0:q_rows] += comb[q]
         part_y[q].start()
+
+    def x_rows():
+        spread_ids(1)
+        flip_rows(4, 1)
 
     scores(sb0, 0)
 
@@ -310,22 +319,29 @@
                 if then is not None:
                     then()
 
-        on(3, [*feat_p, ids_p])
-        on(7, [feat_x[0], feat_y[0], feat_y[1], ids_y, ids_yp, ids_xn], [pass_p[0], pass_p[1]],
-           then=functools.partial(spread_ids, 1))
-        on(9, [pass_p[0], pass_p[1], feat_y[2]], [pass_p[2]])
-        on(10, [pass_p[2], feat_y[3]], [pass_p[3]])
-        on(11, [pass_p[3]])
-        on(13, feat_x[1:], [part_x[0]])
-        on(16, (), [part_c[0]])
-        on(17, then=functools.partial(join, 0))
-        on(20, (), [part_x[1]])
-        on(23, (), [part_c[1]])
-        on(24, then=functools.partial(join, 1))
-        on(26, (), [part_x[2]])
-        on(28, (), [part_c[2]])
-        on(29, then=functools.partial(join, 2))
-        on(31, (), [part_x[3], *part_p])
+        on(1, [*feat_p, ids_p])
+        on(3, [feat_x[0], ids_xn], then=x_rows)
+        on(4, [feat_y[0], ids_y, ids_yp], [pass_p[0]])
+        on(5, [pass_p[0]])
+        on(6, [feat_y[1]], [pass_p[1]])
+        on(7, [feat_x[1]], then=functools.partial(flip_rows, 5, 1))
+        on(8, [feat_y[2]], [pass_p[2]])
+        on(10, [feat_x[2]], then=functools.partial(flip_rows, 6, 1))
+        on(11, [feat_x[3], feat_y[3], pass_p[1]], [pass_p[3]], then=functools.partial(flip_rows, 7, 1))
+        on(12, [pass_p[2], pass_p[3]])
+        on(13, (), [part_c[0]])
+        on(14, (), [part_x[0]], then=functools.partial(join, 0))
+        on(16, (), [part_x[1]])
+        on(19, (), [part_c[1]])
+        on(20, then=functools.partial(join, 1))
+        on(22, (), [part_c[2]])
+        on(23, then=functools.partial(join, 2))
+        on(24, (), [part_x[2]])
+        on(26, (), [part_p[0]])
+        on(27, (), [part_x[3]])
+        on(29, (), [part_c[3]])
+        on(30, then=functools.partial(join, 3))
+        on(31, (), [part_p[1]])
 
         t = 2 * f
         scores(sb1, t + 1)
@@ -336,13 +352,11 @@
         gradients(gb0, t)
 
     gradients(gb1, n_tiles - 1)
-    part_c[3].start()
     outs = [pltpu.make_async_copy(di.at[pl.ds(0, rows)], d_img, own_sem.at[0]),
-            pltpu.make_async_copy(dt.at[0], d_txt.at[pl.ds(0, COL_BLK)], own_sem.at[1]),
-            pltpu.make_async_copy(dt.at[1], d_txt.at[pl.ds(COL_BLK, COL_BLK)], own_sem.at[2])]
+            pltpu.make_async_copy(dt.at[0], d_txt.at[:, pl.ds(0, COL_BLK)], own_sem.at[1]),
+            pltpu.make_async_copy(dt.at[1], d_txt.at[:, pl.ds(COL_BLK, COL_BLK)], own_sem.at[2])]
     for cp in outs:
         cp.start()
-    join(3)
     for cp in outs:
         cp.wait()
     for cp in (*part_x, *part_p, *part_y):
@@ -355,19 +369,20 @@
     rows, width = emb_img.shape
     hbm = pl.BlockSpec(memory_space=pl.ANY)
     vmem = pl.BlockSpec(memory_space=pltpu.VMEM)
-    grads = jax.ShapeDtypeStruct((rows, width), F32)
+    grads, grads_t = jax.ShapeDtypeStruct((rows, width), F32), jax.ShapeDtypeStruct((width, rows), F32)
     return pl.pallas_call(
         pair_kernel,
         name="pair_grads",
-        out_shape=(grads, grads, grads, grads, grads, jax.ShapeDtypeStruct((4, 8, COL_BLK), F32)),
+        out_shape=(grads, grads_t, grads, grads_t, grads_t, jax.ShapeDtypeStruct((4, 8, COL_BLK), F32)),
         in_specs=[pl.BlockSpec(memory_space=pltpu.SMEM), hbm, hbm, hbm, hbm, hbm],
         out_specs=(hbm, hbm, hbm, hbm, hbm, vmem),
         scratch_shapes=[
             pltpu.VMEM((2 * rows, width), BF16),
+            pltpu.VMEM((8, width, ROW_BLK), BF16),
             pltpu.VMEM((8, COL_BLK, width), BF16),
             pltpu.VMEM((2 * rows, width), F32),
-            pltpu.VMEM((8, COL_BLK, width), F32),
-            pltpu.VMEM((4, rows // 4, width), F32),
+            pltpu.VMEM((8, width, COL_BLK), F32),
+            pltpu.VMEM((4, width, rows // 4), F32),
             pltpu.VMEM((2 * rows, 128), jnp.int32),
             pltpu.VMEM((8, 1, COL_BLK), jnp.int32),
             pltpu.VMEM((2, rows // 128, 128), jnp.int32),

time: 310 us -> 246 us (0.79)
  Pallas kernels: 295 us -> 231 us
    pallas_call x1, Pallas kernels: 235 us -> 170 us  [pair_grads(): pl.pallas_call(pair_kernel, name='pair_grads', out_shape=(grads, grads_t,...]
where the time goes in v3:
time: 246 us
  Pallas kernels  231 us (94%)
  between operations  7.97 us (3%)
  local copies, waits for them, and re-layouts  5.53 us (2%)
    pallas_call x1, Pallas kernels, pair_grads(): pl.pallas_call(pair_kernel, name='pair_grads', out_shape=(grads, grads_t,...  170 us
    pallas_call x1, Pallas kernels, all_reduce(): pl.pallas_call(reduce_kernel, name='all_reduce', out_shape=(jax.ShapeDtyp...  37.7 us
    pallas_call x1, Pallas kernels, weight_grads(): pl.pallas_call(weight_kernel, name='weight_grads', grid=(rows // blk,), o...  16 us
    pallas_call x1, Pallas kernels, embed(): pl.pallas_call(embed_kernel, name='embed', grid=(rows // blk,), out_shape...  6.9 us

profile of v3, /device:TPU:0, one launch (start us, length us, event | category | flops | bytes accessed | tf_op | source)
XLA Modules:
  0.0 245.8 jit_solution(4779129905623337682)
XLA Ops:
  2.0 0.6 pad_maximum_fusion.coef
  2.5 6.9 %embed.1 = (bf16[2048,512]{1,0:T(8,128)(2,1)}, bf16[2048,512]{1,0:T(8,128)(2,1)}) custom-call(bf16[2048,768]{1,0:T(8,128)(2,1)} %x_img.3, bf16[2048,512]{1,0:T(8,128)(2,1)} %x_txt.3, bf16[768,512]{1,0:T(8,128)(2,1)} %w_img.3, bf16[512,512]{1,0:T(8,128)(2,1)} %w_txt.3), custom_call_target="tpu_custom_call" | custom-call | tf_op jit(solution)/shard_map/embed/pallas_call | solution.py:45
  9.5 170.3 %pair_grads.1 = (f32[2048,512]{1,0:T(8,128)}, f32[512,2048]{1,0:T(8,128)}, f32[2048,512]{1,0:T(8,128)}, f32[512,2048]{1,0:T(8,128)}, f32[512,2048]{1,0:T(8,128)}, /*index=5*/f32[4,8,1024]{2,1,0:T(8,128)}) custom-call(f32[2]{0:T(128)} %pad_maximum_fusion.coef, bf16[2048,512]{1,0:T(8,128)(2,1)} %get-tuple-element.17.emb_img, ...), custom_call_target="tpu_custom_call" | custom-call | tf_op jit(solution)/shard_map/pair_grads/pallas_call | solution.py:373
  179.7 16.0 %weight_grads.1 = (f32[1280,512]{1,0:T(8,128)}, f32[8,512]{1,0:T(8,128)}) custom-call(f32[1]{0:T(128)} %bitcast.scale, bf16[2048,768]{1,0:T(8,128)(2,1)} %x_img.3, bf16[2048,512]{1,0:T(8,128)(2,1)} %x_txt.3, bf16[768,512]{1,0:T(8,128)(2,1)} %w_img.3, bf16[512,512]{1,0:T(8,128)(2,1)} %w_txt.3, f32[2048,512]{1,0:T(8,128)} %get-tuple-element.19.d_img, ...), custom_call_target="tpu_custom_call" | custom-call | tf_op jit(solution)/shard_map/weight_grads/pallas_call | solution.py:83
  195.7 37.7 %all_reduce.1 = (f32[1280,512]{1,0:T(8,128)}, f32[8,512]{1,0:T(8,128)}) custom-call(f32[1280,512]{1,0:T(8,128)} %get-tuple-element.25.x, f32[8,512]{1,0:T(8,128)} %get-tuple-element.26.part), custom_call_target="tpu_custom_call" | custom-call | tf_op jit(solution)/shard_map/all_reduce/pallas_call | solution.py:159
  233.4 0.7 reduce_sum.10
  234.1 0.1 bitcast_reduce_fusion
  234.3 0.6 fusion
  237.5 2.3 slice.23
  239.7 2.7 %slice.22 = f32[768,512]{1,0:T(8,128)} slice(f32[1280,512]{1,0:T(8,128)} %get-tuple-element.28), slice={[0:768], [0:512]} | slice | bytes 3145728 | tf_op jit(solution)/shard_map/slice | solution.py:416
